TPU v7x, 512 devices: a whole 4x4x16 slice. The times are simulated.
512 devices in a mesh: gx: 8 (over x, core), gy: 8 (over z_lo), gz: 8 (over z_hi, y).
Axes of the slice: x: 4, y: 4, z: 16 (z_hi: 2, z_lo: 8; z = z_hi * 8 + z_lo), core: 2. Of those that a mesh axis runs over, the one named last changes fastest.
Arguments:
- attn_out: bfloat16 [1408, 8192], P('gx', ('gz', 'gy')), may hold values from -6 to 6
- residual: bfloat16 [1408, 8192], P('gx', ('gy', 'gz')), may hold values from -60 to 60
- proj_weight: bfloat16 [8192, 8192], P(('gz', 'gx'), 'gy'), may hold values from -0.0625 to 0.0625
- norm_gain: float32 [8192], P(('gy', 'gz')), may hold values from 0.1 to 1.9
- gate_proj: bfloat16 [8192, 14336], P(('gy', 'gx'), 'gz'), may hold values from -0.0625 to 0.0625
- up_proj: bfloat16 [8192, 14336], P(('gy', 'gx'), 'gz'), may hold values from -0.0625 to 0.0625
- down_proj: bfloat16 [14336, 8192], P(('gz', 'gx'), 'gy'), may hold values from -0.046875 to 0.046875
Outputs:
- layer_out: bfloat16 [1408, 8192], P('gx', ('gy', 'gz'))
All inputs are finite; a program needn't handle non-finite values.
Results may differ from a plain program's by a relative error of at most 0.0029.
Values may be sent and summed in bfloat16 or wider, within the bound.
A program may use at most 64 MiB of HBM per device.

v0:
```python
import jax
import jax.numpy as jnp
from jax import lax
from jax.sharding import Mesh
from jax.sharding import PartitionSpec as P

D = 8192
GX = ("gx_0", "gx_1")
GZ_GX = ("gz", "gx_0", "gx_1")
GY_GX = ("gy", "gx_0", "gx_1")


def in_order(parts, dim):
    shape = list(parts.shape[1:])
    shape[dim] *= parts.shape[0]
    return jnp.moveaxis(parts, 0, dim).reshape(shape)


def from_everyone(value, axis):
    copies = jnp.broadcast_to(value, (lax.axis_size(axis), *value.shape))
    return lax.all_to_all(copies, axis, split_axis=0, concat_axis=0, tiled=True)


def gather_directly(value, axis, dim):
    return in_order(from_everyone(value, axis), dim)


def split_up(value, dim, size):
    shape = value.shape
    parts = value.reshape(*shape[:dim], size, shape[dim] // size, *shape[dim + 1 :])
    return jnp.moveaxis(parts, dim, 0)


def summed_on_arrival(value, axis, dim):
    parts = split_up(value, dim, lax.axis_size(axis))
    arrived = lax.all_to_all(parts, axis, split_axis=0, concat_axis=0, tiled=True)
    return arrived.sum(axis=0)


def over_copies(value, axis):
    return from_everyone(value, axis).sum(axis=0)


def sent_together(arrays, axis, dim, along):
    ends, at = ([], 0)
    for a in arrays[:-1]:
        at += a.shape[along]
        ends.append(at)
    both = jnp.concatenate(arrays, axis=along)
    return tuple(jnp.split(lax.all_gather(both, axis, axis=dim, tiled=True), ends, axis=along))


def side_by_side(arrays, axis, dim, along):
    widths = [a.shape[along] for a in arrays]
    both = jnp.concatenate(arrays, axis=along)
    whole = lax.psum_scatter(both, axis, scatter_dimension=dim, tiled=True)
    return tuple(jnp.split(whole, [sum(widths[:k]) for k in range(1, len(widths))], axis=along))


def edges_of(length, count):
    hop = length // count
    if hop >= 8:
        hop -= hop % 8
    return [hop * k for k in range(1, count)]


def all_blocks(value, axes, turns):
    parts = value
    for k in turns:
        parts = lax.all_gather(parts, axes[k])
    done = turns[::-1]
    back = [done.index(k) for k in range(len(axes))]
    parts = parts.transpose(*back, *range(len(axes), parts.ndim))
    return parts.reshape(-1, *value.shape)


def spread_gather(value, axes, dim):
    cut = max(range(max(1, value.ndim - 1)), key=lambda d: value.shape[d])
    count, outs = (len(axes), [])
    for initial, share in enumerate(jnp.split(value, edges_of(value.shape[cut], count), axis=cut)):
        if share.size:
            turns = [(initial - k) % count for k in range(count)]
            outs.append(all_blocks(share, axes, turns))
    return in_order(jnp.concatenate(outs, axis=cut + 1), dim)


def add_block(lefts, pieces):
    return jnp.dot(lefts, pieces, preferred_element_type=jnp.float32)


def on_device(attn_out, residual, proj_weight, norm_gain, gate_proj, up_proj, down_proj):
    attn_cols = gather_directly(attn_out, "gy", 1)
    proj_partial = add_block(attn_cols, gather_directly(proj_weight, GX, 0))
    projected = summed_on_arrival(proj_partial, "gz", 1)
    stream = residual.astype(jnp.float32) + projected
    squares = over_copies(jnp.sum(stream * stream, axis=1), ("gy", "gz"))
    scaled = (stream * norm_gain[None, :]).astype(jnp.bfloat16)
    model_cols = gather_directly(scaled, "gz", 1)
    inverse = lax.rsqrt(squares / D + 1e-05)[:, None]
    pieces = sent_together((gate_proj, up_proj), GX, 0, 1)
    gate_part = add_block(model_cols, pieces[0])
    up_part = add_block(model_cols, pieces[1])
    gate_sum, up_sum = side_by_side((gate_part, up_part), "gy", 1, 0)
    hidden = (jax.nn.silu(inverse * gate_sum) * (inverse * up_sum)).astype(jnp.bfloat16)
    hidden_cols = gather_directly(hidden, "gy", 1)
    down_partial = add_block(hidden_cols, spread_gather(down_proj, GX, 0))
    down_sum = summed_on_arrival(down_partial, "gz", 1)
    return (stream + down_sum).astype(jnp.bfloat16)


def solution(mesh):
    split = Mesh(
        mesh.devices.reshape(4, 2, mesh.shape["gy"], mesh.shape["gz"]), ("gx_0", "gx_1", "gy", "gz")
    )
    in_specs = (
        P(GX, ("gz", "gy")),
        P(GX, ("gy", "gz")),
        P(GZ_GX, "gy"),
        P(("gy", "gz")),
        P(GY_GX, "gz"),
        P(GY_GX, "gz"),
        P(GZ_GX, "gy"),
    )
    out_specs = P(GX, ("gy", "gz"))
    return jax.shard_map(
        on_device, mesh=split, in_specs=in_specs, out_specs=out_specs, check_vma=False
    )
```

profile of v0, /device:TPU:6, one launch (start us, length us, event | category | flops | bytes accessed | tf_op | source)
XLA Modules:
  0.0 355.8 jit_solution(11354125520535368602)
XLA Ops:
  7.4 2.2 pad_maximum_fusion.2
  9.6 0.8 broadcast_in_dim.17
  10.4 12.5 %all-to-all-start = ((bf16[8,176,128]{2,1,0:T(8,128)(2,1)}), bf16[8,176,128]{2,1,0:T(8,128)(2,1)S(1)}, u32[]{:S(2)}, u32[]{:S(2)}) async-start(bf16[8,176,128]{2,1,0:T(8,128)(2,1)} %broadcast_in_dim.17), calls=%async_computation | async-start | bytes 720896 | tf_op jit(solution)/shard_map/all_to_all | solution.py:21
  23.1 21.5 %all-to-all-done = bf16[8,176,128]{2,1,0:T(8,128)(2,1)S(1)} async-done(((bf16[8,176,128]{2,1,0:T(8,128)(2,1)}), bf16[8,176,128]{2,1,0:T(8,128)(2,1)S(1)}, u32[]{:S(2)}, u32[]{:S(2)}) %all-to-all-start) | async-done | bytes 360480 | tf_op jit(solution)/shard_map/all_to_all | solution.py:21
  44.6 1.7 broadcast_in_dim.18
  46.3 4.8 %all-to-all-start.1 = ((bf16[8,128,1024]{1,2,0:T(8,128)(2,1)}), bf16[8,128,1024]{1,2,0:T(8,128)(2,1)S(1)}, u32[]{:S(2)}, u32[]{:S(2)}) async-start(bf16[8,128,1024]{1,2,0:T(8,128)(2,1)} %broadcast_in_dim.18), calls=%async_computation.1 | async-start | bytes 4194304 | tf_op jit(solution)/shard_map/all_to_all | solution.py:21
  51.3 36.3 %all-to-all-done.1 = bf16[8,128,1024]{1,2,0:T(8,128)(2,1)S(1)} async-done(((bf16[8,128,1024]{1,2,0:T(8,128)(2,1)}), bf16[8,128,1024]{1,2,0:T(8,128)(2,1)S(1)}, u32[]{:S(2)}, u32[]{:S(2)}) %all-to-all-start.1) | async-done | bytes 2097184 | tf_op jit(solution)/shard_map/all_to_all | solution.py:21
  87.6 2.6 copy.42
  90.3 2.9 copy.43
  93.2 0.8 convolution_bitcast_fusion.1
  94.0 49.3 %all_to_all.36 = f32[8,176,128]{2,1,0:T(8,128)S(1)} all-to-all(f32[8,176,128]{2,1,0:T(8,128)S(1)} %convolution_bitcast_fusion.1), channel_id=1, replica_groups=mesh['gx_0'=4,'gx_1'=2,'gy'=8,'gz'=8] {'gz'}, dimensions={0} | all-to-all | bytes 1441792 | tf_op jit(solution)/shard_map/all_to_all | solution.py:36
  143.5 24.2 %all_to_all.37 = bf16[8,176,128]{2,1,0:T(8,128)(2,1)S(1)} all-to-all(bf16[8,176,128]{2,1,0:T(8,128)(2,1)S(1)} %broadcast_in_dim.20), channel_id=1, replica_groups=mesh['gx_0'=4,'gx_1'=2,'gy'=8,'gz'=8] {'gz'}, dimensions={0} | all-to-all | bytes 720896 | tf_op jit(solution)/shard_map/all_to_all | solution.py:21
  167.7 2.9 fusion
  170.6 2.9 fusion.2
  173.6 2.2 copy.49
  175.9 0.9 copy-done
  176.8 14.3 %all-gather = bf16[448,1024]{1,0:T(8,128)(2,1)} all-gather(bf16[112,1024]{1,0:T(8,128)(2,1)S(1)} %get-tuple-element.5), channel_id=2, replica_groups=mesh['gx_0'=4,'gx_1'=2,'gy'=8,'gz'=8] {'gx_0'}, dimensions={0}, use_global_device_ids=true | all-gather | bytes 1146880 | tf_op jit(solution)/shard_map/all_gather | solution.py:70
  191.2 0.7 broadcast_in_dim.19
  191.8 13.2 %all-to-all-start.3 = ((f32[64,1,176]{2,1,0:T(1,128)}), f32[64,1,176]{2,1,0:T(1,128)S(1)}, u32[]{:S(2)}, u32[]{:S(2)}) async-start(f32[64,1,176]{2,1,0:T(1,128)} %broadcast_in_dim.19), calls=%async_computation.3 | async-start | bytes 131072 | tf_op jit(solution)/shard_map/all_to_all | solution.py:21
  205.1 2.3 all-gather.2
  207.4 13.2 %all-to-all-done.3 = f32[64,1,176]{2,1,0:T(1,128)S(1)} async-done(((f32[64,1,176]{2,1,0:T(1,128)}), f32[64,1,176]{2,1,0:T(1,128)S(1)}, u32[]{:S(2)}, u32[]{:S(2)}) %all-to-all-start.3) | async-done | bytes 45088 | tf_op jit(solution)/shard_map/all_to_all | solution.py:21
  220.7 33.6 %reduce-scatter.4.cloned.1.call-done = f32[224,352]{1,0:T(8,128)} async-done(((f32[1792,352]{1,0:T(8,128)}), f32[224,352]{1,0:T(8,128)}) %reduce-scatter.4.cloned.1.call-update) | async-done | bytes 315408
  254.3 1.2 fusion.9
  255.8 0.9 broadcast_in_dim.21
  256.7 5.8 %all-to-all-start.5 = ((bf16[8,176,224]{2,1,0:T(8,128)(2,1)}), bf16[8,176,224]{2,1,0:T(8,128)(2,1)S(1)}, u32[]{:S(2)}, u32[]{:S(2)}) async-start(bf16[8,176,224]{2,1,0:T(8,128)(2,1)} %broadcast_in_dim.21), calls=%async_computation.5 | async-start | bytes 1441792 | tf_op jit(solution)/shard_map/all_to_all | solution.py:21
  262.5 1.7 copy.47
  264.3 3.9 %pad_maximum_fusion = bf16[8,224,1024]{2,1,0:T(8,128)(2,1)} fusion(bf16[8,112,1024]{2,1,0:T(8,128)(2,1)} %all-gather.12.cloned.1.call-done, bf16[8,112,1024]{2,1,0:T(8,128)(2,1)S(1)} %bitcast.44), kind=kLoop, calls=%fused_computation.4 | loop fusion | flops 7340032 | bytes 7340032 | tf_op jit(solution)/shard_map/concatenate | solution.py:84
  268.2 6.0 %copy.48 = bf16[1024,1792]{1,0:T(8,128)(2,1)} copy(bf16[1024,1792]{0,1:T(8,128)(2,1)} %bitcast.40) | data formatting | bytes 7340032 | tf_op jit(solution)/shard_map/dot_general | solution.py:88
  274.1 23.6 %all-to-all-done.5 = bf16[8,176,224]{2,1,0:T(8,128)(2,1)S(1)} async-done(((bf16[8,176,224]{2,1,0:T(8,128)(2,1)}), bf16[8,176,224]{2,1,0:T(8,128)(2,1)S(1)}, u32[]{:S(2)}, u32[]{:S(2)}) %all-to-all-start.5) | async-done | bytes 630816 | tf_op jit(solution)/shard_map/all_to_all | solution.py:21
  297.9 0.9 reshape.48
  298.8 3.4 convolution_bitcast_fusion
  302.2 45.5 %all_to_all.38 = f32[8,176,128]{2,1,0:T(8,128)S(1)} all-to-all(f32[8,176,128]{2,1,0:T(8,128)S(1)} %convolution_bitcast_fusion), channel_id=1, replica_groups=mesh['gx_0'=4,'gx_1'=2,'gy'=8,'gz'=8] {'gz'}, dimensions={0} | all-to-all | bytes 1441792 | tf_op jit(solution)/shard_map/all_to_all | solution.py:36
  (36 shorter events, 2.4 us)
Async XLA Ops:
  7.4 2.2 copy-start.3
  7.4 15.5 %copy-start.1 = (bf16[128,1024]{1,0:T(8,128)(2,1)S(1)}, bf16[128,1024]{1,0:T(8,128)(2,1)}, u32[]{:S(2)}) copy-start(bf16[128,1024]{1,0:T(8,128)(2,1)} %param.9) | copy-start | bytes 786436
  7.4 160.3 %all-gather.8.cloned.1.call-start = ((), (), s32[]{:S(2)}) async-start(), calls=%async_computation.8 | async-start | bytes 8257536 | tf_op jit(solution)/shard_map/all_gather | solution.py:50
  10.4 34.2 %all-to-all-start = ((bf16[8,176,128]{2,1,0:T(8,128)(2,1)}), bf16[8,176,128]{2,1,0:T(8,128)(2,1)S(1)}, u32[]{:S(2)}, u32[]{:S(2)}) async-start(bf16[8,176,128]{2,1,0:T(8,128)(2,1)} %broadcast_in_dim.17), calls=%async_computation | async-start | bytes 720896 | tf_op jit(solution)/shard_map/all_to_all | solution.py:21
  46.3 41.4 %all-to-all-start.1 = ((bf16[8,128,1024]{1,2,0:T(8,128)(2,1)}), bf16[8,128,1024]{1,2,0:T(8,128)(2,1)S(1)}, u32[]{:S(2)}, u32[]{:S(2)}) async-start(bf16[8,128,1024]{1,2,0:T(8,128)(2,1)} %broadcast_in_dim.18), calls=%async_computation.1 | async-start | bytes 4194304 | tf_op jit(solution)/shard_map/all_to_all | solution.py:21
  51.1 203.2 %reduce-scatter.4.cloned.1.call-start = ((), (), s32[]{:S(2)}) async-start(), calls=%async_computation.11 | async-start | bytes 3096576
  93.1 50.2 %copy-start.2 = (bf16[176,128]{1,0:T(8,128)(2,1)S(1)}, bf16[176,128]{1,0:T(8,128)(2,1)}, u32[]{:S(2)}) copy-start(bf16[176,128]{1,0:T(8,128)(2,1)} %param.8) | copy-start | bytes 135172
  93.1 50.2 %copy-start.4 = (f32[128]{0:T(128)S(1)}, f32[128]{0:T(128)}, u32[]{:S(2)}) copy-start(f32[128]{0:T(128)} %param.10) | copy-start | bytes 1540
  175.8 1.0 copy-start
  175.8 86.7 %all-gather.10.cloned.1.call-start = ((), (), s32[]{:S(2)}) async-start(), calls=%async_computation.9 | async-start | bytes 2752512 | tf_op jit(solution)/shard_map/all_gather | solution.py:70
  191.8 28.7 %all-to-all-start.3 = ((f32[64,1,176]{2,1,0:T(1,128)}), f32[64,1,176]{2,1,0:T(1,128)S(1)}, u32[]{:S(2)}, u32[]{:S(2)}) async-start(f32[64,1,176]{2,1,0:T(1,128)} %broadcast_in_dim.19), calls=%async_computation.3 | async-start | bytes 131072 | tf_op jit(solution)/shard_map/all_to_all | solution.py:21
  205.0 59.2 %all-gather.12.cloned.1.call-start = ((), (), s32[]{:S(2)}) async-start(), calls=%async_computation.10 | async-start | bytes 2293760 | tf_op jit(solution)/shard_map/all_gather | solution.py:70
  256.7 41.0 %all-to-all-start.5 = ((bf16[8,176,224]{2,1,0:T(8,128)(2,1)}), bf16[8,176,224]{2,1,0:T(8,128)(2,1)S(1)}, u32[]{:S(2)}, u32[]{:S(2)}) async-start(bf16[8,176,224]{2,1,0:T(8,128)(2,1)} %broadcast_in_dim.21), calls=%async_computation.5 | async-start | bytes 1441792 | tf_op jit(solution)/shard_map/all_to_all | solution.py:21
Sparse Core Ops, SparseCore 0:
  10.3 70.9 all-gather.7
  175.9 78.2 reduce-scatter.3
Sparse Core Ops, SparseCore 1:
  191.3 19.1 all-gather.9
  212.4 35.9 all-gather.11
where the time goes:
time: 363 us; the launch traced here: 356 us
  blocking collectives  136 us (37%)
  waiting for transfers between devices  128 us (35%)
  starting transfers between devices  36.3 us (10%)
  local copies, waits for them, and re-layouts  23.3 us (6%)
  between operations  15 us (4%)
  matrix products  9.93 us (3%)
  other arithmetic  7.31 us (2%)
    all_to_all x2, blocking collectives, summed_on_arrival(): lax.all_to_all(parts, axis, split_axis=0, concat_axis=0, tiled=True)  94.8 us
    all_to_all x4, waiting for transfers between devices, from_everyone(): return lax.all_to_all(copies, axis, split_axis=0, concat_axis=0, tiled=True)  94.6 us
    all_to_all x4, starting transfers between devices, from_everyone(): return lax.all_to_all(copies, axis, split_axis=0, concat_axis=0, tiled=True)  36.2 us
    unnamed x5, waiting for transfers between devices  33.7 us
    all_to_all x1, blocking collectives, from_everyone(): return lax.all_to_all(copies, axis, split_axis=0, concat_axis=0, tiled=True)  24.2 us
    all_gather x2, blocking collectives, all_blocks(): parts = lax.all_gather(parts, axes[k])  16.6 us
    dot_general x4, matrix products, add_block(): return jnp.dot(lefts, pieces, preferred_element_type=jnp.float32)  9.93 us
    dot_general x2, local copies, waits for them, and re-layouts, add_block(): return jnp.dot(lefts, pieces, preferred_element_type=jnp.float32)  8.82 us
  transfers between devices with their start and end apart: 8, of which 5 were waited for; matrix products, arithmetic and copies ran while one was open for 7% of the time, Pallas kernels for 0%

commit v1 on v0

v1 whole, which is shorter than its diff:
```python
import jax
import jax.numpy as jnp
from jax import lax
from jax.experimental import pallas as pl
from jax.experimental.pallas import tpu as pltpu
from jax.sharding import PartitionSpec as P

MESH = pl.DeviceIdType.MESH
D = 8192
ROWS, TILE = 176, 128
UNITS, UNIT = 7, 256
F32, BF16 = jnp.float32, jnp.bfloat16
X_STEPS = (2, 6, 4)


def rcopy(src, dst, send, recv, **where):
    return pltpu.make_async_remote_copy(
        src_ref=src, dst_ref=dst, send_sem=send, recv_sem=recv, device_id=where, device_id_type=MESH
    )


def signal(sem, **where):
    pl.semaphore_signal(sem, inc=1, device_id=where, device_id_type=MESH)


def dot(a, b):
    return jnp.dot(a, b, preferred_element_type=F32)


def kernel(
    attn_ref, res_ref, gain_ref, wp_hbm, wg_hbm, wu_hbm, wd_hbm, out_ref,
    attn_all, wp, wg, wu, wd, part8, y_send, y_recv, zh_send, zh_recv,
    gain_recv, stream, scaled, ssq_y, ssq_gy, inv, gu, acc_r, acc_l, hid, down,
    w_local, w_send, w_recv, w_fsend, w_frecv, a_send, a_recv, ys_send, ys_recv, ya_send, ya_recv,
    sy_send, sy_recv, sg_send, sg_recv, z_send, z_recv, r_send, r_recv, l_send, l_recv,
    hr_send, hl_send, h_recv,
):
    gx, gy, gz = lax.axis_index("gx"), lax.axis_index("gy"), lax.axis_index("gz")
    mate = gx + 1 - 2 * lax.rem(gx, 2)
    y, zh = lax.rem(gz, 4), gz // 4
    across = lax.rem(gz + 4, 8)
    up_chip, down_chip = lax.min(gy + 1, 7), lax.max(gy - 1, 0)

    weights = ((wp_hbm, wp), (wg_hbm, wg), (wu_hbm, wu), (wd_hbm, wd))

    def rows_of(w, who):
        depth = weights[w][0].shape[0]
        return weights[w][1].at[pl.ds(pl.multiple_of(who * depth, 16), depth)]

    def own_copy(w):
        return pltpu.make_async_copy(weights[w][0], rows_of(w, gx), w_local.at[w])

    for w in range(4):
        own_copy(w).start()

    barrier = pltpu.get_barrier_semaphore()
    for step in X_STEPS:
        signal(barrier, gx=lax.rem(gx + step, 8))
    signal(barrier, gx=mate)
    for d in range(1, 8):
        signal(barrier, gy=lax.rem(gy + d, 8))
    for d in range(1, 4):
        signal(barrier, gz=zh * 4 + lax.rem(y + d, 4))
    signal(barrier, gz=across)
    pl.semaphore_wait(barrier, 15)

    def attn_copy(d):
        return rcopy(attn_ref, attn_all.at[gy], a_send.at[d], a_recv.at[d], gy=lax.rem(gy + d, 8))

    def attn_arrival(d):
        who = lax.rem(gy + 8 - d, 8)
        return rcopy(attn_ref, attn_all.at[who], a_send.at[d], a_recv.at[d], gy=who)

    for d in range(1, 8):
        attn_copy(d).start()

    def w_copy(w, k):
        who = lax.rem(gx + X_STEPS[k], 8)
        return rcopy(weights[w][0], rows_of(w, gx), w_send.at[w, k], w_recv.at[w, k], gx=who)

    def w_arrival(w, k):
        who = lax.rem(gx + 8 - X_STEPS[k], 8)
        return rcopy(weights[w][0], rows_of(w, who), w_send.at[w, k], w_recv.at[w, k], gx=who)

    def w_mate(w, k):
        who = gx if k == 3 else lax.rem(gx + 8 - X_STEPS[k], 8)
        src = weights[w][0] if k == 3 else rows_of(w, who)
        return rcopy(src, rows_of(w, who), w_fsend.at[w, k], w_frecv.at[w, k], gx=mate)

    def w_mate_arrival(w, k):
        who = mate if k == 3 else lax.rem(mate + 8 - X_STEPS[k], 8)
        dst = rows_of(w, who)
        return rcopy(dst, dst, w_fsend.at[w, k], w_frecv.at[w, k], gx=mate)

    for w in range(4):
        for k in range(3):
            w_copy(w, k).start()
        w_mate(w, 3).start()

    def gain_copy():
        return rcopy(gain_ref, gain_recv, z_send.at[0], z_recv.at[0], gz=across)

    gain_copy().start()

    def forward(w):
        for k in range(3):
            w_arrival(w, k).wait_recv()
            w_mate(w, k).start()

    def weights_here(w):
        for k in range(4):
            w_mate_arrival(w, k).wait_recv()
        own_copy(w).wait()

    def y_copy(n, d):
        who = lax.rem(y + d, 4)
        return rcopy(
            y_send.at[n, who], y_recv.at[n, d - 1], ys_send.at[n, d - 1], ys_recv.at[n, d - 1],
            gz=zh * 4 + who,
        )

    def keep_tiles(n, m, total):
        for half in range(2):
            block = 2 * m + half
            tile = total[:, half * TILE : (half + 1) * TILE]
            part8[block] = tile
            y_send[n, block % 4, block // 4] = tile.astype(BF16)

    def y_sum(n, side):
        total = part8[side * 4 + y]
        for d in range(3):
            total += y_recv[n, d, side].astype(F32)
        return total

    attn_all[gy] = attn_ref[...]
    forward(0)
    for d in range(1, 8):
        attn_arrival(d).wait_recv()
    weights_here(0)
    for m in range(4):
        total = None
        for k in range(4):
            left = jnp.concatenate([attn_all[2 * k], attn_all[2 * k + 1]], axis=1)
            term = dot(left, wp[k * 256 : (k + 1) * 256, m * 256 : (m + 1) * 256])
            total = term if total is None else total + term
        keep_tiles(0, m, total)
    for d in range(1, 4):
        y_copy(0, d).start()
    for d in range(1, 4):
        y_copy(0, d).wait_recv()

    def zh_copy():
        return rcopy(zh_send.at[pl.ds(0, 2)], zh_recv.at[pl.ds(0, 2)], z_send.at[1], z_recv.at[1], gz=across)

    mine = res_ref[...].astype(F32) + y_sum(0, zh)
    theirs = y_sum(0, 1 - zh)
    zh_send[0] = mine.astype(BF16)
    zh_send[1] = theirs.astype(BF16)
    zh_copy().start()
    forward(1)
    gain_copy().wait_recv()
    zh_copy().wait_recv()
    mine += zh_recv[1].astype(F32)
    theirs += zh_recv[0].astype(F32)
    stream[...] = mine
    scaled[y, zh] = (mine * gain_ref[...]).astype(BF16)
    scaled[y, 1 - zh] = (theirs * gain_recv[...]).astype(BF16)

    def scaled_copy(d):
        who = zh * 4 + lax.rem(y + d, 4)
        return rcopy(scaled.at[y], scaled.at[y], ya_send.at[d], ya_recv.at[d], gz=who)

    def scaled_arrival(d):
        who = lax.rem(y + 4 - d, 4)
        return rcopy(scaled.at[who], scaled.at[who], ya_send.at[d], ya_recv.at[d], gz=zh * 4 + who)

    def ssq_copy(d):
        who = zh * 4 + lax.rem(y + d, 4)
        return rcopy(ssq_y.at[0], ssq_y.at[d], sy_send.at[d], sy_recv.at[d], gz=who)

    def ssq_gy_copy(d):
        who = lax.rem(gy + d, 8)
        return rcopy(ssq_gy.at[0], ssq_gy.at[d], sg_send.at[d], sg_recv.at[d], gy=who)

    for d in range(1, 4):
        scaled_copy(d).start()
    squares = jnp.sum(mine * mine + theirs * theirs, axis=1, keepdims=True)
    squares = jnp.concatenate(
        [jnp.broadcast_to(squares, (ROWS, TILE)), jnp.zeros((256 - ROWS, TILE), F32)], axis=0
    )
    ssq_y[0] = squares.T[:8]
    for d in range(1, 4):
        ssq_copy(d).start()
    for d in range(1, 4):
        scaled_arrival(d).wait_recv()
        ssq_copy(d).wait_recv()
    ssq_gy[0] = ssq_y[0] + ssq_y[1] + ssq_y[2] + ssq_y[3]
    for d in range(1, 8):
        ssq_gy_copy(d).start()

    forward(2)
    weights_here(1)
    weights_here(2)

    def products(unit):
        columns = pl.ds(pl.multiple_of(unit * UNIT, UNIT), UNIT)
        for part, w in enumerate((wg, wu)):
            total = None
            for k in range(4):
                a, b = 2 * k, 2 * k + 1
                left = jnp.concatenate([scaled[a % 4, a // 4], scaled[b % 4, b // 4]], axis=1)
                term = dot(left, w[k * 256 : (k + 1) * 256, columns])
                total = term if total is None else total + term
            gu[unit, part] = total

    def r_copy(unit, part):
        return rcopy(
            acc_r.at[unit, part], acc_r.at[unit, part], r_send.at[unit, part], r_recv.at[unit, part],
            gy=up_chip,
        )

    def l_copy(unit, part):
        return rcopy(
            acc_l.at[unit, part], acc_l.at[unit, part], l_send.at[unit, part], l_recv.at[unit, part],
            gy=down_chip,
        )

    def pass_on(unit, copy, acc, first):
        for part in range(2):

            @pl.when(first)
            def _():
                acc[unit, part] = gu[unit, part].astype(BF16)

            @pl.when(jnp.logical_not(first))
            def _():
                copy(unit, part).wait_recv()
                acc[unit, part] = (gu[unit, part] + acc[unit, part].astype(F32)).astype(BF16)

            copy(unit, part).start()

    def owner_of(unit):
        return unit + lax.min(lax.max(unit - 3, 0), 1)

    def line_step(t, carry):
        @pl.when(t < 4)
        def _():
            products(6 - t)

        @pl.when(t < 3)
        def _():
            products(t)

        right = 6 - t + gy

        @pl.when(jnp.logical_and(t >= gy, owner_of(right) > gy))
        def _():
            pass_on(right, r_copy, acc_r, gy == 0)

        left = t - 7 + gy

        @pl.when(jnp.logical_and(left >= 0, owner_of(left) < gy))
        def _():
            pass_on(left, l_copy, acc_l, gy == 7)

        return carry

    lax.fori_loop(0, 7, line_step, 0)

    for d in range(1, 8):
        ssq_gy_copy(d).wait_recv()
    total = ssq_gy[0]
    for d in range(1, 8):
        total += ssq_gy[d]
    total = lax.rsqrt(total[:1] / D + 1e-05)
    inv[...] = jnp.broadcast_to(total, (TILE, 256)).T

    owns = gy != 4
    own_unit = gy - lax.min(lax.max(gy - 4, 0), 1)

    @pl.when(owns)
    def _():
        for part in range(2):

            @pl.when(gy > 0)
            def _():
                r_copy(own_unit, part).wait_recv()
                gu[own_unit, part] += acc_r[own_unit, part].astype(F32)

            @pl.when(gy < 7)
            def _():
                l_copy(own_unit, part).wait_recv()
                gu[own_unit, part] += acc_l[own_unit, part].astype(F32)

        for half in range(2):
            columns = slice(half * TILE, (half + 1) * TILE)
            gate = inv[:ROWS] * gu[own_unit, 0, :, columns]
            up = inv[:ROWS] * gu[own_unit, 1, :, columns]
            hid[own_unit, half] = (gate / (1.0 + jnp.exp(-gate)) * up).astype(BF16)

    forward(3)
    weights_here(3)

    def hr_copy(unit, half):
        block = hid.at[unit, half]
        return rcopy(block, block, hr_send.at[unit, half], h_recv.at[unit, half], gy=up_chip)

    def hl_copy(unit, half):
        block = hid.at[unit, half]
        return rcopy(block, block, hl_send.at[unit, half], h_recv.at[unit, half], gy=down_chip)

    def add_down(unit):
        left = jnp.concatenate([hid[unit, 0], hid[unit, 1]], axis=1)
        rows = pl.ds(pl.multiple_of(unit * UNIT, UNIT), UNIT)
        for m in range(4):
            down[m] += dot(left, wd[rows, m * 256 : (m + 1) * 256])

    down[...] = jnp.zeros_like(down)

    @pl.when(owns)
    def _():
        for half in range(2):

            @pl.when(gy < 7)
            def _():
                hr_copy(own_unit, half).start()

            @pl.when(gy > 0)
            def _():
                hl_copy(own_unit, half).start()

        add_down(own_unit)

    def hidden_step(t, carry):
        from_left, from_right = gy - t, gy + t
        left_unit = from_left - lax.min(lax.max(from_left - 4, 0), 1)
        right_unit = from_right - lax.min(lax.max(from_right - 4, 0), 1)
        has_left = jnp.logical_and(from_left >= 0, from_left != 4)
        has_right = jnp.logical_and(from_right <= 7, from_right != 4)
        for has, unit, copy, more in (
            (has_left, left_unit, hr_copy, gy < 7), (has_right, right_unit, hl_copy, gy > 0)
        ):

            @pl.when(has)
            def _():
                for half in range(2):
                    copy(unit, half).wait_recv()

                    @pl.when(more)
                    def _():
                        copy(unit, half).start()

        for has, unit in ((has_left, left_unit), (has_right, right_unit)):

            @pl.when(has)
            def _():
                add_down(unit)

        return carry

    lax.fori_loop(1, 8, hidden_step, 0)

    for m in range(4):
        keep_tiles(1, m, down[m])
    for d in range(1, 4):
        y_copy(1, d).start()
    for d in range(1, 4):
        y_copy(1, d).wait_recv()

    def last_copy():
        return rcopy(zh_send.at[2], zh_recv.at[2], z_send.at[2], z_recv.at[2], gz=across)

    zh_send[2] = y_sum(1, 1 - zh).astype(BF16)
    last_copy().start()
    stream[...] += y_sum(1, zh)
    last_copy().wait_recv()
    out_ref[...] = (stream[...] + zh_recv[2].astype(F32)).astype(BF16)

    for d in range(1, 8):
        attn_copy(d).wait_send()
        ssq_gy_copy(d).wait_send()
    for w in range(4):
        for k in range(3):
            w_copy(w, k).wait_send()
            w_mate(w, k).wait_send()
        w_mate(w, 3).wait_send()
    for d in range(1, 4):
        y_copy(0, d).wait_send()
        y_copy(1, d).wait_send()
        scaled_copy(d).wait_send()
        ssq_copy(d).wait_send()
    gain_copy().wait_send()
    zh_copy().wait_send()
    last_copy().wait_send()

    def drain(unit, carry):
        owner = owner_of(unit)
        for part in range(2):

            @pl.when(owner > gy)
            def _():
                r_copy(unit, part).wait_send()

            @pl.when(owner < gy)
            def _():
                l_copy(unit, part).wait_send()

            @pl.when(jnp.logical_and(owner <= gy, gy < 7))
            def _():
                hr_copy(unit, part).wait_send()

            @pl.when(jnp.logical_and(owner >= gy, gy > 0))
            def _():
                hl_copy(unit, part).wait_send()

        return carry

    lax.fori_loop(0, UNITS, drain, 0)


def on_device(attn_out, residual, proj_weight, norm_gain, gate_proj, up_proj, down_proj):
    tile = (ROWS, TILE)
    in_vmem, in_hbm = pl.BlockSpec(memory_space=pltpu.VMEM), pl.BlockSpec(memory_space=pl.ANY)
    dma = pltpu.SemaphoreType.DMA
    return pl.pallas_call(
        kernel,
        out_shape=jax.ShapeDtypeStruct(tile, BF16),
        in_specs=[in_vmem] * 3 + [in_hbm] * 4,
        out_specs=in_vmem,
        scratch_shapes=[
            pltpu.VMEM((8, *tile), BF16),
            pltpu.VMEM((1024, 1024), BF16),
            pltpu.VMEM((1024, 1792), BF16),
            pltpu.VMEM((1024, 1792), BF16),
            pltpu.VMEM((1792, 1024), BF16),
            pltpu.VMEM((8, *tile), F32),
            pltpu.VMEM((2, 4, 2, *tile), BF16),
            pltpu.VMEM((2, 3, 2, *tile), BF16),
            pltpu.VMEM((3, *tile), BF16),
            pltpu.VMEM((3, *tile), BF16),
            pltpu.VMEM((1, TILE), F32),
            pltpu.VMEM(tile, F32),
            pltpu.VMEM((4, 2, *tile), BF16),
            pltpu.VMEM((4, 8, 256), F32),
            pltpu.VMEM((8, 8, 256), F32),
            pltpu.VMEM((256, TILE), F32),
            pltpu.VMEM((UNITS, 2, ROWS, UNIT), F32),
            pltpu.VMEM((UNITS, 2, ROWS, UNIT), BF16),
            pltpu.VMEM((UNITS, 2, ROWS, UNIT), BF16),
            pltpu.VMEM((UNITS, 2, *tile), BF16),
            pltpu.VMEM((4, ROWS, 256), F32),
            dma((4,)), dma((4, 3)), dma((4, 3)), dma((4, 4)), dma((4, 4)),
            dma((8,)), dma((8,)), dma((2, 3)), dma((2, 3)), dma((4,)), dma((4,)),
            dma((4,)), dma((4,)), dma((8,)), dma((8,)), dma((3,)), dma((3,)),
            dma((UNITS, 2)), dma((UNITS, 2)), dma((UNITS, 2)), dma((UNITS, 2)),
            dma((UNITS, 2)), dma((UNITS, 2)), dma((UNITS, 2)),
        ],
        compiler_params=pltpu.CompilerParams(
            collective_id=0, has_side_effects=True, vmem_limit_bytes=56 << 20
        ),
    )(attn_out, residual, norm_gain.reshape(1, TILE), proj_weight, gate_proj, up_proj, down_proj)


def solution(mesh):
    in_specs = (
        P("gx", ("gz", "gy")),
        P("gx", ("gy", "gz")),
        P(("gz", "gx"), "gy"),
        P(("gy", "gz")),
        P(("gy", "gx"), "gz"),
        P(("gy", "gx"), "gz"),
        P(("gz", "gx"), "gy"),
    )
    return jax.shard_map(
        on_device, mesh=mesh, in_specs=in_specs, out_specs=P("gx", ("gy", "gz")), check_vma=False
    )
```

time: 363 us -> 149 us (0.41); the launches traced: 356 us -> 147 us
  Pallas kernels: 0 us -> 146 us
  blocking collectives: 136 us -> 0 us
  waiting for transfers between devices: 128 us -> 0 us
  starting transfers between devices: 36.3 us -> 0 us
  local copies, waits for them, and re-layouts: 23.3 us -> 1.41 us
  between operations: 15 us -> 0.01 us
  matrix products: 9.93 us -> 0 us
  other arithmetic: 7.31 us -> 0 us
    pallas_call x0 -> x1, Pallas kernels: none -> 146 us  [on_device(): pl.pallas_call(kernel, out_shape=jax.ShapeDtypeStruct(tile, BF16), in_spe...]
    all_to_all x3 -> x0, blocking collectives: 119 us -> none  [the longest x2 94.8 us: summed_on_arrival(): lax.all_to_all(parts, axis, split_axis=0, concat_axis=0, tiled=True)]
    all_to_all x4 -> x0, waiting for transfers between devices: 94.6 us -> none  [from_everyone(): return lax.all_to_all(copies, axis, split_axis=0, concat_axis=0, tiled=True)]
    all_to_all x4 -> x0, starting transfers between devices: 36.2 us -> none  [from_everyone(): return lax.all_to_all(copies, axis, split_axis=0, concat_axis=0, tiled=True)]
    unnamed x5 -> x0, waiting for transfers between devices: 33.7 us -> none
    all_gather x2 -> x0, blocking collectives: 16.6 us -> none  [all_blocks(): parts = lax.all_gather(parts, axes[k])]
    dot_general x4 -> x0, matrix products: 9.93 us -> none  [add_block(): return jnp.dot(lefts, pieces, preferred_element_type=jnp.float32)]
    dot_general x2 -> x0, local copies, waits for them, and re-layouts: 8.82 us -> none  [add_block(): return jnp.dot(lefts, pieces, preferred_element_type=jnp.float32)]
  transfers between devices with their start and end apart: 8 -> 0, of which waited for: 5 -> 0; matrix products, arithmetic and copies ran while one was open for 7% -> 0% of each run, Pallas kernels for 0% -> 0%
where the time goes in v1:
time: 149 us; the launch traced here: 147 us
  Pallas kernels  146 us (98%)
    pallas_call x1, Pallas kernels, on_device(): pl.pallas_call(kernel, out_shape=jax.ShapeDtypeStruct(tile, BF16), in_spe...  146 us

profile of v1, /device:TPU:6, one launch (start us, length us, event | category | flops | bytes accessed | tf_op | source)
XLA Modules:
  0.0 147.2 jit_solution(11687380487953971693)
XLA Ops:
  0.0 145.8 %shard_map.73 = bf16[176,128]{1,0:T(8,128)(2,1)} custom-call(bf16[176,128]{1,0:T(8,128)(2,1)} %attn_ref.1, bf16[176,128]{1,0:T(8,128)(2,1)} %res_ref.1, f32[1,128]{1,0:T(1,128)} %bitcast.1, bf16[128,1024]{1,0:T(8,128)(2,1)} %wp_hbm.1, bf16[128,1792]{1,0:T(8,128)(2,1)} %wg_hbm.1, bf16[128,1792]{1,0:T(8,128)(2,1)} %wu_hbm.1, bf16[224,1024]{1,0:T(8,128)(2,1)} %wd_hbm.1), custom_call_target="tpu_custom_call" | custom-call | tf_op jit(solution)/shard_map/pallas_call | solution.py:425
  145.8 1.4 copy.9

commit v2 on v1

--- a/solution.py
+++ b/solution.py
@@ -11,6 +11,7 @@
 UNITS, UNIT = 7, 256
 F32, BF16 = jnp.float32, jnp.bfloat16
 X_STEPS = (2, 6, 4)
+PIECES = ((0, 96), (96, 80))
 
 
 def rcopy(src, dst, send, recv, **where):
@@ -31,7 +32,7 @@
     attn_ref, res_ref, gain_ref, wp_hbm, wg_hbm, wu_hbm, wd_hbm, out_ref,
     attn_all, wp, wg, wu, wd, part8, y_send, y_recv, zh_send, zh_recv,
     gain_recv, stream, scaled, ssq_y, ssq_gy, inv, gu, acc_r, acc_l, hid, down,
-    w_local, w_send, w_recv, w_fsend, w_frecv, a_send, a_recv, ys_send, ys_recv, ya_send, ya_recv,
+    w_local, w_send, w_recv, w_psend, w_fsend, w_frecv, ar_send, al_send, a_recv, hello, ys_send, ys_recv, ya_send, ya_recv,
     sy_send, sy_recv, sg_send, sg_recv, z_send, z_recv, r_send, r_recv, l_send, l_recv,
     hr_send, hl_send, h_recv,
 ):
@@ -53,34 +54,76 @@
     for w in range(4):
         own_copy(w).start()
 
+    ahead = dict(gy=lax.rem(gy + 1, 8), gz=lax.select(gy == 7, across, gz))
+    behind = dict(gy=lax.rem(gy + 7, 8), gz=lax.select(gy == 0, across, gz))
     barrier = pltpu.get_barrier_semaphore()
     for step in X_STEPS:
         signal(barrier, gx=lax.rem(gx + step, 8))
     signal(barrier, gx=mate)
-    for d in range(1, 8):
-        signal(barrier, gy=lax.rem(gy + d, 8))
     for d in range(1, 4):
         signal(barrier, gz=zh * 4 + lax.rem(y + d, 4))
-    signal(barrier, gz=across)
-    pl.semaphore_wait(barrier, 15)
-
-    def attn_copy(d):
-        return rcopy(attn_ref, attn_all.at[gy], a_send.at[d], a_recv.at[d], gy=lax.rem(gy + d, 8))
-
-    def attn_arrival(d):
-        who = lax.rem(gy + 8 - d, 8)
-        return rcopy(attn_ref, attn_all.at[who], a_send.at[d], a_recv.at[d], gy=who)
-
-    for d in range(1, 8):
-        attn_copy(d).start()
-
-    def w_copy(w, k):
+    signal(barrier, **ahead)
+    signal(barrier, **behind)
+    pl.semaphore_wait(barrier, 9)
+    signal(hello, **ahead)
+
+    def attn_copy(block, piece, own, send, who):
+        rows = pl.ds(*PIECES[piece])
+        src = attn_ref.at[rows] if own else attn_all.at[block, rows]
+        return rcopy(src, attn_all.at[block, rows], send.at[block, piece], a_recv.at[block, piece], gy=who)
+
+    def ar_copy(block, piece, own=False):
+        return attn_copy(block, piece, own, ar_send, up_chip)
+
+    def al_copy(block, piece, own=False):
+        return attn_copy(block, piece, own, al_send, down_chip)
+
+    for piece in range(2):
+
+        @pl.when(gy < 7)
+        def _():
+            ar_copy(gy, piece, True).start()
+
+        @pl.when(gy > 0)
+        def _():
+            al_copy(gy, piece, True).start()
+
+    def half_of(w, who, half):
+        depth = weights[w][0].shape[0] // 2
+        return weights[w][1].at[pl.ds(pl.multiple_of((2 * who + half) * depth, 16), depth)]
+
+    def own_half(w, half):
+        depth = weights[w][0].shape[0] // 2
+        return weights[w][0].at[pl.ds(half * depth, depth)]
+
+    def p_copy(k):
         who = lax.rem(gx + X_STEPS[k], 8)
-        return rcopy(weights[w][0], rows_of(w, gx), w_send.at[w, k], w_recv.at[w, k], gx=who)
-
-    def w_arrival(w, k):
+        return rcopy(wp_hbm, rows_of(0, gx), w_psend.at[k, 0], w_psend.at[k, 1], gx=who)
+
+    def p_arrival(k):
         who = lax.rem(gx + 8 - X_STEPS[k], 8)
-        return rcopy(weights[w][0], rows_of(w, who), w_send.at[w, k], w_recv.at[w, k], gx=who)
+        return rcopy(wp_hbm, rows_of(0, who), w_psend.at[k, 0], w_psend.at[k, 1], gx=who)
+
+    def w_copy(w, k, half):
+        who = lax.rem(gx + X_STEPS[k], 8)
+        return rcopy(
+            own_half(w, half), half_of(w, gx, half), w_send.at[w - 1, k, half], w_recv.at[w - 1, k, half], gx=who
+        )
+
+    def w_arrival(w, k, half):
+        who = lax.rem(gx + 8 - X_STEPS[k], 8)
+        dst = half_of(w, who, half)
+        return rcopy(dst, dst, w_send.at[w - 1, k, half], w_recv.at[w - 1, k, half], gx=who)
+
+    def w_onward(w, half):
+        origin, who = lax.rem(gx + 8 - X_STEPS[half], 8), lax.rem(gx + X_STEPS[half], 8)
+        block = half_of(w, origin, half)
+        return rcopy(block, block, w_send.at[w - 1, 2, half], w_recv.at[w - 1, 2, half], gx=who)
+
+    def w_onward_arrival(w, half):
+        block = half_of(w, lax.rem(gx + 4, 8), half)
+        who = lax.rem(gx + 8 - X_STEPS[half], 8)
+        return rcopy(block, block, w_send.at[w - 1, 2, half], w_recv.at[w - 1, 2, half], gx=who)
 
     def w_mate(w, k):
         who = gx if k == 3 else lax.rem(gx + 8 - X_STEPS[k], 8)
@@ -92,25 +135,71 @@
         dst = rows_of(w, who)
         return rcopy(dst, dst, w_fsend.at[w, k], w_frecv.at[w, k], gx=mate)
 
+    def send_own(w):
+        for half in range(2):
+            w_copy(w, 0, half).start()
+            w_copy(w, 1, 1 - half).start()
+
+    for k in range(3):
+        p_copy(k).start()
+    send_own(1)
+    send_own(2)
     for w in range(4):
-        for k in range(3):
-            w_copy(w, k).start()
         w_mate(w, 3).start()
 
-    def gain_copy():
-        return rcopy(gain_ref, gain_recv, z_send.at[0], z_recv.at[0], gz=across)
-
-    gain_copy().start()
-
-    def forward(w):
-        for k in range(3):
-            w_arrival(w, k).wait_recv()
+    def pass_weights(w):
+        for half in range(2):
+            w_arrival(w, half, half).wait_recv()
+            w_onward(w, half).start()
+        for k in range(2):
+            w_arrival(w, k, 1 - k).wait_recv()
             w_mate(w, k).start()
+
+    def last_weights(w):
+        for half in range(2):
+            w_onward_arrival(w, half).wait_recv()
+        w_mate(w, 2).start()
 
     def weights_here(w):
         for k in range(4):
             w_mate_arrival(w, k).wait_recv()
         own_copy(w).wait()
+
+    def attn_step(t, carry):
+        for piece in range(2):
+            for has, block, copy, more in (
+                (gy >= t, gy - t, ar_copy, gy < 7), (gy + t <= 7, gy + t, al_copy, gy > 0)
+            ):
+
+                @pl.when(has)
+                def _():
+                    copy(block, piece).wait_recv()
+
+                    @pl.when(more)
+                    def _():
+                        copy(block, piece).start()
+
+        pl.semaphore_wait(hello, 1)
+        signal(hello, **ahead)
+
+        @pl.when(t == 5)
+        def _():
+            for k in range(2):
+                p_arrival(k).wait_recv()
+                w_mate(0, k).start()
+
+        return carry
+
+    attn_all[gy] = attn_ref[...]
+    lax.fori_loop(1, 8, attn_step, 0)
+    p_arrival(2).wait_recv()
+    w_mate(0, 2).start()
+    pl.semaphore_wait(hello, 1)
+
+    def gain_copy():
+        return rcopy(gain_ref, gain_recv, z_send.at[0], z_recv.at[0], gz=across)
+
+    gain_copy().start()
 
     def y_copy(n, d):
         who = lax.rem(y + d, 4)
@@ -132,10 +221,6 @@
             total += y_recv[n, d, side].astype(F32)
         return total
 
-    attn_all[gy] = attn_ref[...]
-    forward(0)
-    for d in range(1, 8):
-        attn_arrival(d).wait_recv()
     weights_here(0)
     for m in range(4):
         total = None
@@ -146,6 +231,7 @@
         keep_tiles(0, m, total)
     for d in range(1, 4):
         y_copy(0, d).start()
+    pass_weights(1)
     for d in range(1, 4):
         y_copy(0, d).wait_recv()
 
@@ -157,7 +243,9 @@
     zh_send[0] = mine.astype(BF16)
     zh_send[1] = theirs.astype(BF16)
     zh_copy().start()
-    forward(1)
+    pass_weights(2)
+    send_own(3)
+    last_weights(1)
     gain_copy().wait_recv()
     zh_copy().wait_recv()
     mine += zh_recv[1].astype(F32)
@@ -191,14 +279,14 @@
     ssq_y[0] = squares.T[:8]
     for d in range(1, 4):
         ssq_copy(d).start()
+    last_weights(2)
     for d in range(1, 4):
         scaled_arrival(d).wait_recv()
         ssq_copy(d).wait_recv()
-    ssq_gy[0] = ssq_y[0] + ssq_y[1] + ssq_y[2] + ssq_y[3]
+    ssq_gy[0] = (ssq_y[0] + ssq_y[1] + ssq_y[2] + ssq_y[3])[:1]
     for d in range(1, 8):
         ssq_gy_copy(d).start()
 
-    forward(2)
     weights_here(1)
     weights_here(2)
 
@@ -211,7 +299,8 @@
                 left = jnp.concatenate([scaled[a % 4, a // 4], scaled[b % 4, b // 4]], axis=1)
                 term = dot(left, w[k * 256 : (k + 1) * 256, columns])
                 total = term if total is None else total + term
-            gu[unit, part] = total
+            for half in range(2):
+                gu[unit, 2 * part + half] = total[:, half * TILE : (half + 1) * TILE]
 
     def r_copy(unit, part):
         return rcopy(
@@ -225,19 +314,17 @@
             gy=down_chip,
         )
 
-    def pass_on(unit, copy, acc, first):
-        for part in range(2):
-
-            @pl.when(first)
-            def _():
-                acc[unit, part] = gu[unit, part].astype(BF16)
-
-            @pl.when(jnp.logical_not(first))
-            def _():
-                copy(unit, part).wait_recv()
-                acc[unit, part] = (gu[unit, part] + acc[unit, part].astype(F32)).astype(BF16)
-
-            copy(unit, part).start()
+    def pass_on(tile, unit, copy, acc, first):
+        @pl.when(first)
+        def _():
+            acc[unit, tile] = gu[unit, tile].astype(BF16)
+
+        @pl.when(jnp.logical_not(first))
+        def _():
+            copy(unit, tile).wait_recv()
+            acc[unit, tile] = (gu[unit, tile] + acc[unit, tile].astype(F32)).astype(BF16)
+
+        copy(unit, tile).start()
 
     def owner_of(unit):
         return unit + lax.min(lax.max(unit - 3, 0), 1)
@@ -245,23 +332,30 @@
     def line_step(t, carry):
         @pl.when(t < 4)
         def _():
-            products(6 - t)
+            products(lax.select(gy < 4, 6 - t, t))
+
+        right, left = 6 - t + gy, t - 7 + gy
+        for tile in range(4):
+
+            @pl.when(jnp.logical_and(t >= gy, owner_of(right) > gy))
+            def _():
+                pass_on(tile, right, r_copy, acc_r, gy == 0)
+
+            @pl.when(jnp.logical_and(left >= 0, owner_of(left) < gy))
+            def _():
+                pass_on(tile, left, l_copy, acc_l, gy == 7)
 
         @pl.when(t < 3)
         def _():
-            products(t)
-
-        right = 6 - t + gy
-
-        @pl.when(jnp.logical_and(t >= gy, owner_of(right) > gy))
-        def _():
-            pass_on(right, r_copy, acc_r, gy == 0)
-
-        left = t - 7 + gy
-
-        @pl.when(jnp.logical_and(left >= 0, owner_of(left) < gy))
-        def _():
-            pass_on(left, l_copy, acc_l, gy == 7)
+            products(lax.select(gy < 4, t, 6 - t))
+
+        @pl.when(t == 2)
+        def _():
+            pass_weights(3)
+
+        @pl.when(t == 5)
+        def _():
+            last_weights(3)
 
         return carry
 
@@ -272,7 +366,7 @@
     total = ssq_gy[0]
     for d in range(1, 8):
         total += ssq_gy[d]
-    total = lax.rsqrt(total[:1] / D + 1e-05)
+    total = lax.rsqrt(total / D + 1e-05)
     inv[...] = jnp.broadcast_to(total, (TILE, 256)).T
 
     owns = gy != 4
@@ -280,34 +374,35 @@
 
     @pl.when(owns)
     def _():
-        for part in range(2):
+        for tile in range(4):
 
             @pl.when(gy > 0)
             def _():
-                r_copy(own_unit, part).wait_recv()
-                gu[own_unit, part] += acc_r[own_unit, part].astype(F32)
+                r_copy(own_unit, tile).wait_recv()
+                gu[own_unit, tile] += acc_r[own_unit, tile].astype(F32)
 
             @pl.when(gy < 7)
             def _():
-                l_copy(own_unit, part).wait_recv()
-                gu[own_unit, part] += acc_l[own_unit, part].astype(F32)
+                l_copy(own_unit, tile).wait_recv()
+                gu[own_unit, tile] += acc_l[own_unit, tile].astype(F32)
 
         for half in range(2):
-            columns = slice(half * TILE, (half + 1) * TILE)
-            gate = inv[:ROWS] * gu[own_unit, 0, :, columns]
-            up = inv[:ROWS] * gu[own_unit, 1, :, columns]
+            gate = inv[:ROWS] * gu[own_unit, half]
+            up = inv[:ROWS] * gu[own_unit, 2 + half]
             hid[own_unit, half] = (gate / (1.0 + jnp.exp(-gate)) * up).astype(BF16)
 
-    forward(3)
     weights_here(3)
 
-    def hr_copy(unit, half):
-        block = hid.at[unit, half]
-        return rcopy(block, block, hr_send.at[unit, half], h_recv.at[unit, half], gy=up_chip)
-
-    def hl_copy(unit, half):
-        block = hid.at[unit, half]
-        return rcopy(block, block, hl_send.at[unit, half], h_recv.at[unit, half], gy=down_chip)
+    def hidden_copy(unit, k, send, who):
+        half, piece = k // 2, k % 2
+        block = hid.at[unit, half, pl.ds(*PIECES[piece])]
+        return rcopy(block, block, send.at[unit, k], h_recv.at[unit, k], gy=who)
+
+    def hr_copy(unit, k):
+        return hidden_copy(unit, k, hr_send, up_chip)
+
+    def hl_copy(unit, k):
+        return hidden_copy(unit, k, hl_send, down_chip)
 
     def add_down(unit):
         left = jnp.concatenate([hid[unit, 0], hid[unit, 1]], axis=1)
@@ -319,15 +414,15 @@
 
     @pl.when(owns)
     def _():
-        for half in range(2):
+        for k in range(4):
 
             @pl.when(gy < 7)
             def _():
-                hr_copy(own_unit, half).start()
+                hr_copy(own_unit, k).start()
 
             @pl.when(gy > 0)
             def _():
-                hl_copy(own_unit, half).start()
+                hl_copy(own_unit, k).start()
 
         add_down(own_unit)
 
@@ -337,18 +432,18 @@
         right_unit = from_right - lax.min(lax.max(from_right - 4, 0), 1)
         has_left = jnp.logical_and(from_left >= 0, from_left != 4)
         has_right = jnp.logical_and(from_right <= 7, from_right != 4)
-        for has, unit, copy, more in (
-            (has_left, left_unit, hr_copy, gy < 7), (has_right, right_unit, hl_copy, gy > 0)
-        ):
-
-            @pl.when(has)
-            def _():
-                for half in range(2):
-                    copy(unit, half).wait_recv()
+        for k in range(4):
+            for has, unit, copy, more in (
+                (has_left, left_unit, hr_copy, gy < 7), (has_right, right_unit, hl_copy, gy > 0)
+            ):
+
+                @pl.when(has)
+                def _():
+                    copy(unit, k).wait_recv()
 
                     @pl.when(more)
                     def _():
-                        copy(unit, half).start()
+                        copy(unit, k).start()
 
         for has, unit in ((has_left, left_unit), (has_right, right_unit)):
 
@@ -377,13 +472,17 @@
     out_ref[...] = (stream[...] + zh_recv[2].astype(F32)).astype(BF16)
 
     for d in range(1, 8):
-        attn_copy(d).wait_send()
         ssq_gy_copy(d).wait_send()
+    for k in range(3):
+        p_copy(k).wait_send()
     for w in range(4):
-        for k in range(3):
-            w_copy(w, k).wait_send()
+        for k in range(4):
             w_mate(w, k).wait_send()
-        w_mate(w, 3).wait_send()
+    for w in range(1, 4):
+        for half in range(2):
+            w_copy(w, 0, half).wait_send()
+            w_copy(w, 1, half).wait_send()
+            w_onward(w, half).wait_send()
     for d in range(1, 4):
         y_copy(0, d).wait_send()
         y_copy(1, d).wait_send()
@@ -395,27 +494,42 @@
 
     def drain(unit, carry):
         owner = owner_of(unit)
-        for part in range(2):
+        for k in range(4):
 
             @pl.when(owner > gy)
             def _():
-                r_copy(unit, part).wait_send()
+                r_copy(unit, k).wait_send()
 
             @pl.when(owner < gy)
             def _():
-                l_copy(unit, part).wait_send()
+                l_copy(unit, k).wait_send()
 
             @pl.when(jnp.logical_and(owner <= gy, gy < 7))
             def _():
-                hr_copy(unit, part).wait_send()
+                hr_copy(unit, k).wait_send()
 
             @pl.when(jnp.logical_and(owner >= gy, gy > 0))
             def _():
-                hl_copy(unit, part).wait_send()
+                hl_copy(unit, k).wait_send()
 
         return carry
 
     lax.fori_loop(0, UNITS, drain, 0)
+
+    def drain_attn(block, carry):
+        for piece in range(2):
+
+            @pl.when(jnp.logical_and(block <= gy, gy < 7))
+            def _():
+                ar_copy(block, piece).wait_send()
+
+            @pl.when(jnp.logical_and(block >= gy, gy > 0))
+            def _():
+                al_copy(block, piece).wait_send()
+
+        return carry
+
+    lax.fori_loop(0, 8, drain_attn, 0)
 
 
 def on_device(attn_out, residual, proj_weight, norm_gain, gate_proj, up_proj, down_proj):
@@ -442,18 +556,19 @@
             pltpu.VMEM(tile, F32),
             pltpu.VMEM((4, 2, *tile), BF16),
             pltpu.VMEM((4, 8, 256), F32),
-            pltpu.VMEM((8, 8, 256), F32),
+            pltpu.VMEM((8, 1, 256), F32),
             pltpu.VMEM((256, TILE), F32),
-            pltpu.VMEM((UNITS, 2, ROWS, UNIT), F32),
-            pltpu.VMEM((UNITS, 2, ROWS, UNIT), BF16),
-            pltpu.VMEM((UNITS, 2, ROWS, UNIT), BF16),
+            pltpu.VMEM((UNITS, 4, *tile), F32),
+            pltpu.VMEM((UNITS, 4, *tile), BF16),
+            pltpu.VMEM((UNITS, 4, *tile), BF16),
             pltpu.VMEM((UNITS, 2, *tile), BF16),
             pltpu.VMEM((4, ROWS, 256), F32),
-            dma((4,)), dma((4, 3)), dma((4, 3)), dma((4, 4)), dma((4, 4)),
-            dma((8,)), dma((8,)), dma((2, 3)), dma((2, 3)), dma((4,)), dma((4,)),
+            dma((4,)), dma((3, 3, 2)), dma((3, 3, 2)), dma((3, 2)), dma((4, 4)), dma((4, 4)),
+            dma((8, 2)), dma((8, 2)), dma((8, 2)), pltpu.SemaphoreType.REGULAR,
+            dma((2, 3)), dma((2, 3)), dma((4,)), dma((4,)),
             dma((4,)), dma((4,)), dma((8,)), dma((8,)), dma((3,)), dma((3,)),
-            dma((UNITS, 2)), dma((UNITS, 2)), dma((UNITS, 2)), dma((UNITS, 2)),
-            dma((UNITS, 2)), dma((UNITS, 2)), dma((UNITS, 2)),
+            dma((UNITS, 4)), dma((UNITS, 4)), dma((UNITS, 4)), dma((UNITS, 4)),
+            dma((UNITS, 4)), dma((UNITS, 4)), dma((UNITS, 4)),
         ],
         compiler_params=pltpu.CompilerParams(
             collective_id=0, has_side_effects=True, vmem_limit_bytes=56 << 20

time: 149 us -> 132 us (0.89)
  Pallas kernels: 146 us -> 130 us
    pallas_call x1, Pallas kernels: 146 us -> 130 us  [on_device(): pl.pallas_call(kernel, out_shape=jax.ShapeDtypeStruct(tile, BF16), in_spe...]
where the time goes in v2:
time: 132 us; the launch traced here: 131 us
  Pallas kernels  130 us (98%)
  local copies, waits for them, and re-layouts  1.41 us (1%)
    pallas_call x1, Pallas kernels, on_device(): pl.pallas_call(kernel, out_shape=jax.ShapeDtypeStruct(tile, BF16), in_spe...  130 us

profile of v2, /device:TPU:6, one launch (start us, length us, event | category | flops | bytes accessed | tf_op | source)
XLA Modules:
  0.0 131.2 jit_solution(5655515392284768977)
XLA Ops:
  0.0 129.8 %shard_map.73 = bf16[176,128]{1,0:T(8,128)(2,1)} custom-call(bf16[176,128]{1,0:T(8,128)(2,1)} %attn_ref.1, bf16[176,128]{1,0:T(8,128)(2,1)} %res_ref.1, f32[1,128]{1,0:T(1,128)} %bitcast.1, bf16[128,1024]{1,0:T(8,128)(2,1)} %wp_hbm.1, bf16[128,1792]{1,0:T(8,128)(2,1)} %wg_hbm.1, bf16[128,1792]{1,0:T(8,128)(2,1)} %wu_hbm.1, bf16[224,1024]{1,0:T(8,128)(2,1)} %wd_hbm.1), custom_call_target="tpu_custom_call" | custom-call | tf_op jit(solution)/shard_map/pallas_call | solution.py:539
  129.8 1.4 %copy.9 = bf16[176,128]{1,0:T(8,128)(2,1)} copy(bf16[176,128]{1,0:T(8,128)(2,1)} %shard_map.73) | data formatting | bytes 90112

commit v3 on v2

--- a/solution.py
+++ b/solution.py
@@ -32,9 +32,9 @@
     attn_ref, res_ref, gain_ref, wp_hbm, wg_hbm, wu_hbm, wd_hbm, out_ref,
     attn_all, wp, wg, wu, wd, part8, y_send, y_recv, zh_send, zh_recv,
     gain_recv, stream, scaled, ssq_y, ssq_gy, inv, gu, acc_r, acc_l, hid, down,
-    w_local, w_send, w_recv, w_psend, w_fsend, w_frecv, ar_send, al_send, a_recv, hello, ys_send, ys_recv, ya_send, ya_recv,
+    w_local, w_send, w_recv, w_fsend, w_frecv, a_send, a_recv, hello, ys_send, ys_recv, ya_send, ya_recv,
     sy_send, sy_recv, sg_send, sg_recv, z_send, z_recv, r_send, r_recv, l_send, l_recv,
-    hr_send, hl_send, h_recv,
+    h_send, h_recv,
 ):
     gx, gy, gz = lax.axis_index("gx"), lax.axis_index("gy"), lax.axis_index("gz")
     mate = gx + 1 - 2 * lax.rem(gx, 2)
@@ -54,39 +54,45 @@
     for w in range(4):
         own_copy(w).start()
 
-    ahead = dict(gy=lax.rem(gy + 1, 8), gz=lax.select(gy == 7, across, gz))
-    behind = dict(gy=lax.rem(gy + 7, 8), gz=lax.select(gy == 0, across, gz))
+    far_gy, quad, place = lax.rem(gy + 4, 8), gy // 4 * 4, lax.rem(gy, 4)
+
+    def in_quad(d):
+        return quad + lax.rem(place + d, 4)
+
     barrier = pltpu.get_barrier_semaphore()
     for step in X_STEPS:
         signal(barrier, gx=lax.rem(gx + step, 8))
     signal(barrier, gx=mate)
     for d in range(1, 4):
         signal(barrier, gz=zh * 4 + lax.rem(y + d, 4))
-    signal(barrier, **ahead)
-    signal(barrier, **behind)
-    pl.semaphore_wait(barrier, 9)
-    signal(hello, **ahead)
-
-    def attn_copy(block, piece, own, send, who):
-        rows = pl.ds(*PIECES[piece])
-        src = attn_ref.at[rows] if own else attn_all.at[block, rows]
-        return rcopy(src, attn_all.at[block, rows], send.at[block, piece], a_recv.at[block, piece], gy=who)
-
-    def ar_copy(block, piece, own=False):
-        return attn_copy(block, piece, own, ar_send, up_chip)
-
-    def al_copy(block, piece, own=False):
-        return attn_copy(block, piece, own, al_send, down_chip)
-
-    for piece in range(2):
-
-        @pl.when(gy < 7)
-        def _():
-            ar_copy(gy, piece, True).start()
-
-        @pl.when(gy > 0)
-        def _():
-            al_copy(gy, piece, True).start()
+        signal(barrier, gy=in_quad(d))
+    signal(barrier, gy=far_gy)
+    signal(barrier, gy=far_gy, gz=across)
+    pl.semaphore_wait(barrier, 12)
+    signal(hello, gy=far_gy, gz=across)
+
+    def attn_far():
+        return rcopy(attn_ref, attn_all.at[gy], a_send.at[0], a_recv.at[0], gy=far_gy)
+
+    def attn_far_arrival():
+        return rcopy(attn_ref, attn_all.at[far_gy], a_send.at[0], a_recv.at[0], gy=far_gy)
+
+    def attn_near(d):
+        return rcopy(attn_ref, attn_all.at[gy], a_send.at[d], a_recv.at[d], gy=in_quad(d))
+
+    def attn_onward(d):
+        block = attn_all.at[far_gy]
+        return rcopy(block, block, a_send.at[3 + d], a_recv.at[3 + d], gy=in_quad(d))
+
+    def attn_arrival(d, onward):
+        who = in_quad(4 - d)
+        block = attn_all.at[lax.rem(who + 4, 8) if onward else who]
+        k = d + 3 if onward else d
+        return rcopy(block, block, a_send.at[k], a_recv.at[k], gy=who)
+
+    attn_far().start()
+    for d in range(1, 4):
+        attn_near(d).start()
 
     def half_of(w, who, half):
         depth = weights[w][0].shape[0] // 2
@@ -96,34 +102,26 @@
         depth = weights[w][0].shape[0] // 2
         return weights[w][0].at[pl.ds(half * depth, depth)]
 
-    def p_copy(k):
-        who = lax.rem(gx + X_STEPS[k], 8)
-        return rcopy(wp_hbm, rows_of(0, gx), w_psend.at[k, 0], w_psend.at[k, 1], gx=who)
-
-    def p_arrival(k):
-        who = lax.rem(gx + 8 - X_STEPS[k], 8)
-        return rcopy(wp_hbm, rows_of(0, who), w_psend.at[k, 0], w_psend.at[k, 1], gx=who)
-
     def w_copy(w, k, half):
         who = lax.rem(gx + X_STEPS[k], 8)
         return rcopy(
-            own_half(w, half), half_of(w, gx, half), w_send.at[w - 1, k, half], w_recv.at[w - 1, k, half], gx=who
+            own_half(w, half), half_of(w, gx, half), w_send.at[w, k, half], w_recv.at[w, k, half], gx=who
         )
 
     def w_arrival(w, k, half):
         who = lax.rem(gx + 8 - X_STEPS[k], 8)
         dst = half_of(w, who, half)
-        return rcopy(dst, dst, w_send.at[w - 1, k, half], w_recv.at[w - 1, k, half], gx=who)
+        return rcopy(dst, dst, w_send.at[w, k, half], w_recv.at[w, k, half], gx=who)
 
     def w_onward(w, half):
         origin, who = lax.rem(gx + 8 - X_STEPS[half], 8), lax.rem(gx + X_STEPS[half], 8)
         block = half_of(w, origin, half)
-        return rcopy(block, block, w_send.at[w - 1, 2, half], w_recv.at[w - 1, 2, half], gx=who)
+        return rcopy(block, block, w_send.at[w, 2, half], w_recv.at[w, 2, half], gx=who)
 
     def w_onward_arrival(w, half):
         block = half_of(w, lax.rem(gx + 4, 8), half)
         who = lax.rem(gx + 8 - X_STEPS[half], 8)
-        return rcopy(block, block, w_send.at[w - 1, 2, half], w_recv.at[w - 1, 2, half], gx=who)
+        return rcopy(block, block, w_send.at[w, 2, half], w_recv.at[w, 2, half], gx=who)
 
     def w_mate(w, k):
         who = gx if k == 3 else lax.rem(gx + 8 - X_STEPS[k], 8)
@@ -135,15 +133,16 @@
         dst = rows_of(w, who)
         return rcopy(dst, dst, w_fsend.at[w, k], w_frecv.at[w, k], gx=mate)
 
-    def send_own(w):
-        for half in range(2):
-            w_copy(w, 0, half).start()
-            w_copy(w, 1, 1 - half).start()
-
-    for k in range(3):
-        p_copy(k).start()
-    send_own(1)
-    send_own(2)
+    def send_own(w, first=True, second=True):
+        if first:
+            w_copy(w, 0, 0).start()
+            w_copy(w, 1, 1).start()
+        if second:
+            w_copy(w, 0, 1).start()
+            w_copy(w, 1, 0).start()
+
+    send_own(0)
+    send_own(1, second=False)
     for w in range(4):
         w_mate(w, 3).start()
 
@@ -165,41 +164,23 @@
             w_mate_arrival(w, k).wait_recv()
         own_copy(w).wait()
 
-    def attn_step(t, carry):
-        for piece in range(2):
-            for has, block, copy, more in (
-                (gy >= t, gy - t, ar_copy, gy < 7), (gy + t <= 7, gy + t, al_copy, gy > 0)
-            ):
-
-                @pl.when(has)
-                def _():
-                    copy(block, piece).wait_recv()
-
-                    @pl.when(more)
-                    def _():
-                        copy(block, piece).start()
-
-        pl.semaphore_wait(hello, 1)
-        signal(hello, **ahead)
-
-        @pl.when(t == 5)
-        def _():
-            for k in range(2):
-                p_arrival(k).wait_recv()
-                w_mate(0, k).start()
-
-        return carry
-
     attn_all[gy] = attn_ref[...]
-    lax.fori_loop(1, 8, attn_step, 0)
-    p_arrival(2).wait_recv()
-    w_mate(0, 2).start()
+    attn_far_arrival().wait_recv()
+    for d in range(1, 4):
+        attn_onward(d).start()
+    pass_weights(0)
+    send_own(1, first=False)
+    send_own(2)
     pl.semaphore_wait(hello, 1)
 
     def gain_copy():
         return rcopy(gain_ref, gain_recv, z_send.at[0], z_recv.at[0], gz=across)
 
     gain_copy().start()
+    for d in range(1, 4):
+        attn_arrival(d, False).wait_recv()
+        attn_arrival(d, True).wait_recv()
+    last_weights(0)
 
     def y_copy(n, d):
         who = lax.rem(y + d, 4)
@@ -393,16 +374,19 @@
 
     weights_here(3)
 
-    def hidden_copy(unit, k, send, who):
+    def hidden_copy(unit, k, side, hop):
         half, piece = k // 2, k % 2
         block = hid.at[unit, half, pl.ds(*PIECES[piece])]
-        return rcopy(block, block, send.at[unit, k], h_recv.at[unit, k], gy=who)
-
-    def hr_copy(unit, k):
-        return hidden_copy(unit, k, hr_send, up_chip)
-
-    def hl_copy(unit, k):
-        return hidden_copy(unit, k, hl_send, down_chip)
+        who = lax.max(lax.min(gy + (1 - 2 * side) * hop, 7), 0)
+        return rcopy(block, block, h_send.at[unit, side, hop - 1, k], h_recv.at[unit, k], gy=who)
+
+    def hidden_sends(unit, k, side, act):
+        room = (7 - gy, gy)[side]
+        for hop in (2, 1):
+
+            @pl.when(room >= hop)
+            def _():
+                act(hidden_copy(unit, k, side, hop))
 
     def add_down(unit):
         left = jnp.concatenate([hid[unit, 0], hid[unit, 1]], axis=1)
@@ -415,45 +399,44 @@
     @pl.when(owns)
     def _():
         for k in range(4):
-
-            @pl.when(gy < 7)
-            def _():
-                hr_copy(own_unit, k).start()
-
-            @pl.when(gy > 0)
-            def _():
-                hl_copy(own_unit, k).start()
+            for side in range(2):
+                hidden_sends(own_unit, k, side, lambda copy: copy.start())
 
         add_down(own_unit)
 
+    def source(side, far):
+        chip = gy - far if side == 0 else gy + far
+        there = jnp.logical_and(jnp.logical_and(chip >= 0, chip <= 7), chip != 4)
+        return there, chip - lax.min(lax.max(chip - 4, 0), 1)
+
     def hidden_step(t, carry):
-        from_left, from_right = gy - t, gy + t
-        left_unit = from_left - lax.min(lax.max(from_left - 4, 0), 1)
-        right_unit = from_right - lax.min(lax.max(from_right - 4, 0), 1)
-        has_left = jnp.logical_and(from_left >= 0, from_left != 4)
-        has_right = jnp.logical_and(from_right <= 7, from_right != 4)
         for k in range(4):
-            for has, unit, copy, more in (
-                (has_left, left_unit, hr_copy, gy < 7), (has_right, right_unit, hl_copy, gy > 0)
-            ):
-
-                @pl.when(has)
+            for side in range(2):
+                there, unit = source(side, 2 * t)
+
+                @pl.when(there)
                 def _():
-                    copy(unit, k).wait_recv()
-
-                    @pl.when(more)
-                    def _():
-                        copy(unit, k).start()
-
-        for has, unit in ((has_left, left_unit), (has_right, right_unit)):
-
-            @pl.when(has)
-            def _():
+                    hidden_copy(unit, k, side, 1).wait_recv()
+                    hidden_sends(unit, k, side, lambda copy: copy.start())
+
+        for side in range(2):
+            there, unit = source(side, 2 * t - 1)
+
+            @pl.when(there)
+            def _():
+                for k in range(4):
+                    hidden_copy(unit, k, side, 1).wait_recv()
                 add_down(unit)
 
+            there, unit = source(side, 2 * t)
+
+            @pl.when(there)
+            def _():
+                add_down(unit)
+
         return carry
 
-    lax.fori_loop(1, 8, hidden_step, 0)
+    lax.fori_loop(1, 5, hidden_step, 0)
 
     for m in range(4):
         keep_tiles(1, m, down[m])
@@ -473,12 +456,14 @@
 
     for d in range(1, 8):
         ssq_gy_copy(d).wait_send()
-    for k in range(3):
-        p_copy(k).wait_send()
+    attn_far().wait_send()
+    for d in range(1, 4):
+        attn_near(d).wait_send()
+        attn_onward(d).wait_send()
     for w in range(4):
         for k in range(4):
             w_mate(w, k).wait_send()
-    for w in range(1, 4):
+    for w in range(4):
         for half in range(2):
             w_copy(w, 0, half).wait_send()
             w_copy(w, 1, half).wait_send()
@@ -504,32 +489,15 @@
             def _():
                 l_copy(unit, k).wait_send()
 
-            @pl.when(jnp.logical_and(owner <= gy, gy < 7))
-            def _():
-                hr_copy(unit, k).wait_send()
-
-            @pl.when(jnp.logical_and(owner >= gy, gy > 0))
-            def _():
-                hl_copy(unit, k).wait_send()
+            for side, far in ((0, gy - owner), (1, owner - gy)):
+
+                @pl.when(jnp.logical_and(far >= 0, lax.rem(far + 8, 2) == 0))
+                def _():
+                    hidden_sends(unit, k, side, lambda copy: copy.wait_send())
 
         return carry
 
     lax.fori_loop(0, UNITS, drain, 0)
-
-    def drain_attn(block, carry):
-        for piece in range(2):
-
-            @pl.when(jnp.logical_and(block <= gy, gy < 7))
-            def _():
-                ar_copy(block, piece).wait_send()
-
-            @pl.when(jnp.logical_and(block >= gy, gy > 0))
-            def _():
-                al_copy(block, piece).wait_send()
-
-        return carry
-
-    lax.fori_loop(0, 8, drain_attn, 0)
 
 
 def on_device(attn_out, residual, proj_weight, norm_gain, gate_proj, up_proj, down_proj):
@@ -563,12 +531,12 @@
             pltpu.VMEM((UNITS, 4, *tile), BF16),
             pltpu.VMEM((UNITS, 2, *tile), BF16),
             pltpu.VMEM((4, ROWS, 256), F32),
-            dma((4,)), dma((3, 3, 2)), dma((3, 3, 2)), dma((3, 2)), dma((4, 4)), dma((4, 4)),
-            dma((8, 2)), dma((8, 2)), dma((8, 2)), pltpu.SemaphoreType.REGULAR,
+            dma((4,)), dma((4, 3, 2)), dma((4, 3, 2)), dma((4, 4)), dma((4, 4)),
+            dma((7,)), dma((7,)), pltpu.SemaphoreType.REGULAR,
             dma((2, 3)), dma((2, 3)), dma((4,)), dma((4,)),
             dma((4,)), dma((4,)), dma((8,)), dma((8,)), dma((3,)), dma((3,)),
             dma((UNITS, 4)), dma((UNITS, 4)), dma((UNITS, 4)), dma((UNITS, 4)),
-            dma((UNITS, 4)), dma((UNITS, 4)), dma((UNITS, 4)),
+            dma((UNITS, 2, 2, 4)), dma((UNITS, 4)),
         ],
         compiler_params=pltpu.CompilerParams(
             collective_id=0, has_side_effects=True, vmem_limit_bytes=56 << 20

time: 132 us -> 124 us (0.939)
  Pallas kernels: 130 us -> 122 us
    pallas_call x1, Pallas kernels: 130 us -> 122 us  [on_device(): pl.pallas_call(kernel, out_shape=jax.ShapeDtypeStruct(tile, BF16), in_spe...]
where the time goes in v3:
time: 124 us; the launch traced here: 123 us
  Pallas kernels  122 us (98%)
  local copies, waits for them, and re-layouts  1.41 us (1%)
    pallas_call x1, Pallas kernels, on_device(): pl.pallas_call(kernel, out_shape=jax.ShapeDtypeStruct(tile, BF16), in_spe...  122 us

profile of v3, /device:TPU:6, one launch (start us, length us, event | category | flops | bytes accessed | tf_op | source)
XLA Modules:
  0.0 123.3 jit_solution(10021965532814179234)
XLA Ops:
  0.0 121.9 %shard_map.73 = bf16[176,128]{1,0:T(8,128)(2,1)} custom-call(bf16[176,128]{1,0:T(8,128)(2,1)} %attn_ref.1, bf16[176,128]{1,0:T(8,128)(2,1)} %res_ref.1, f32[1,128]{1,0:T(1,128)} %bitcast.1, bf16[128,1024]{1,0:T(8,128)(2,1)} %wp_hbm.1, bf16[128,1792]{1,0:T(8,128)(2,1)} %wg_hbm.1, bf16[128,1792]{1,0:T(8,128)(2,1)} %wu_hbm.1, bf16[224,1024]{1,0:T(8,128)(2,1)} %wd_hbm.1), custom_call_target="tpu_custom_call" | custom-call | tf_op jit(solution)/shard_map/pallas_call | solution.py:507
  121.9 1.4 %copy.9 = bf16[176,128]{1,0:T(8,128)(2,1)} copy(bf16[176,128]{1,0:T(8,128)(2,1)} %shard_map.73) | data formatting | bytes 90112

commit v4 on v3

--- a/solution.py
+++ b/solution.py
@@ -42,16 +42,24 @@
     across = lax.rem(gz + 4, 8)
     up_chip, down_chip = lax.min(gy + 1, 7), lax.max(gy - 1, 0)
 
-    weights = ((wp_hbm, wp), (wg_hbm, wg), (wu_hbm, wu), (wd_hbm, wd))
+    pieces = (
+        (wp_hbm, wp, 0, 1024), (wg_hbm, wg, 0, 1024), (wu_hbm, wu, 0, 1024),
+        (wg_hbm, wg, 1024, 768), (wu_hbm, wu, 1024, 768), (wd_hbm, wd, 0, 1024),
+    )
+
+    def own_rows(w):
+        src, _, first, width = pieces[w]
+        return src.at[:, pl.ds(first, width)]
 
     def rows_of(w, who):
-        depth = weights[w][0].shape[0]
-        return weights[w][1].at[pl.ds(pl.multiple_of(who * depth, 16), depth)]
+        src, dst, first, width = pieces[w]
+        depth = src.shape[0]
+        return dst.at[pl.ds(pl.multiple_of(who * depth, 16), depth), pl.ds(first, width)]
 
     def own_copy(w):
-        return pltpu.make_async_copy(weights[w][0], rows_of(w, gx), w_local.at[w])
-
-    for w in range(4):
+        return pltpu.make_async_copy(own_rows(w), rows_of(w, gx), w_local.at[w])
+
+    for w in range(6):
         own_copy(w).start()
 
     far_gy, quad, place = lax.rem(gy + 4, 8), gy // 4 * 4, lax.rem(gy, 4)
@@ -95,12 +103,14 @@
         attn_near(d).start()
 
     def half_of(w, who, half):
-        depth = weights[w][0].shape[0] // 2
-        return weights[w][1].at[pl.ds(pl.multiple_of((2 * who + half) * depth, 16), depth)]
+        src, dst, first, width = pieces[w]
+        depth = src.shape[0] // 2
+        return dst.at[pl.ds(pl.multiple_of((2 * who + half) * depth, 16), depth), pl.ds(first, width)]
 
     def own_half(w, half):
-        depth = weights[w][0].shape[0] // 2
-        return weights[w][0].at[pl.ds(half * depth, depth)]
+        src, _, first, width = pieces[w]
+        depth = src.shape[0] // 2
+        return src.at[pl.ds(half * depth, depth), pl.ds(first, width)]
 
     def w_copy(w, k, half):
         who = lax.rem(gx + X_STEPS[k], 8)
@@ -125,7 +135,7 @@
 
     def w_mate(w, k):
         who = gx if k == 3 else lax.rem(gx + 8 - X_STEPS[k], 8)
-        src = weights[w][0] if k == 3 else rows_of(w, who)
+        src = own_rows(w) if k == 3 else rows_of(w, who)
         return rcopy(src, rows_of(w, who), w_fsend.at[w, k], w_frecv.at[w, k], gx=mate)
 
     def w_mate_arrival(w, k):
@@ -133,17 +143,14 @@
         dst = rows_of(w, who)
         return rcopy(dst, dst, w_fsend.at[w, k], w_frecv.at[w, k], gx=mate)
 
-    def send_own(w, first=True, second=True):
-        if first:
-            w_copy(w, 0, 0).start()
-            w_copy(w, 1, 1).start()
-        if second:
-            w_copy(w, 0, 1).start()
-            w_copy(w, 1, 0).start()
+    def send_own(w):
+        w_copy(w, 0, 0).start()
+        w_copy(w, 1, 1).start()
+        w_copy(w, 0, 1).start()
+        w_copy(w, 1, 0).start()
 
     send_own(0)
-    send_own(1, second=False)
-    for w in range(4):
+    for w in range(6):
         w_mate(w, 3).start()
 
     def pass_weights(w):
@@ -169,7 +176,7 @@
     for d in range(1, 4):
         attn_onward(d).start()
     pass_weights(0)
-    send_own(1, first=False)
+    send_own(1)
     send_own(2)
     pl.semaphore_wait(hello, 1)
 
@@ -213,6 +220,7 @@
     for d in range(1, 4):
         y_copy(0, d).start()
     pass_weights(1)
+    send_own(3)
     for d in range(1, 4):
         y_copy(0, d).wait_recv()
 
@@ -225,8 +233,9 @@
     zh_send[1] = theirs.astype(BF16)
     zh_copy().start()
     pass_weights(2)
-    send_own(3)
+    send_own(4)
     last_weights(1)
+    pass_weights(3)
     gain_copy().wait_recv()
     zh_copy().wait_recv()
     mine += zh_recv[1].astype(F32)
@@ -261,6 +270,8 @@
     for d in range(1, 4):
         ssq_copy(d).start()
     last_weights(2)
+    pass_weights(4)
+    send_own(5)
     for d in range(1, 4):
         scaled_arrival(d).wait_recv()
         ssq_copy(d).wait_recv()
@@ -271,9 +282,13 @@
     weights_here(1)
     weights_here(2)
 
-    def products(unit):
-        columns = pl.ds(pl.multiple_of(unit * UNIT, UNIT), UNIT)
-        for part, w in enumerate((wg, wu)):
+    def place_of(unit):
+        return unit + 2 * lax.min(lax.max(unit - 1, 0), 1) - 5 * lax.min(lax.max(unit - 4, 0), 1)
+
+    def products(unit, parts=(0, 1)):
+        columns = pl.ds(pl.multiple_of(place_of(unit) * UNIT, UNIT), UNIT)
+        for part in parts:
+            w = (wg, wu)[part]
             total = None
             for k in range(4):
                 a, b = 2 * k, 2 * k + 1
@@ -311,12 +326,19 @@
         return unit + lax.min(lax.max(unit - 3, 0), 1)
 
     def line_step(t, carry):
-        @pl.when(t < 4)
-        def _():
-            products(lax.select(gy < 4, 6 - t, t))
-
         right, left = 6 - t + gy, t - 7 + gy
+
+        @pl.when(t == 2)
+        def _():
+            weights_here(3)
+            weights_here(4)
+
         for tile in range(4):
+            if tile % 2 == 0:
+
+                @pl.when(t < 4)
+                def _():
+                    products(lax.select(gy < 4, 6 - t, t), (tile // 2,))
 
             @pl.when(jnp.logical_and(t >= gy, owner_of(right) > gy))
             def _():
@@ -330,13 +352,21 @@
         def _():
             products(lax.select(gy < 4, t, 6 - t))
 
-        @pl.when(t == 2)
-        def _():
-            pass_weights(3)
+        @pl.when(t == 0)
+        def _():
+            last_weights(3)
+
+        @pl.when(t == 1)
+        def _():
+            last_weights(4)
+
+        @pl.when(t == 3)
+        def _():
+            pass_weights(5)
 
         @pl.when(t == 5)
         def _():
-            last_weights(3)
+            last_weights(5)
 
         return carry
 
@@ -372,7 +402,7 @@
             up = inv[:ROWS] * gu[own_unit, 2 + half]
             hid[own_unit, half] = (gate / (1.0 + jnp.exp(-gate)) * up).astype(BF16)
 
-    weights_here(3)
+    weights_here(5)
 
     def hidden_copy(unit, k, side, hop):
         half, piece = k // 2, k % 2
@@ -390,7 +420,7 @@
 
     def add_down(unit):
         left = jnp.concatenate([hid[unit, 0], hid[unit, 1]], axis=1)
-        rows = pl.ds(pl.multiple_of(unit * UNIT, UNIT), UNIT)
+        rows = pl.ds(pl.multiple_of(place_of(unit) * UNIT, UNIT), UNIT)
         for m in range(4):
             down[m] += dot(left, wd[rows, m * 256 : (m + 1) * 256])
 
@@ -460,10 +490,10 @@
     for d in range(1, 4):
         attn_near(d).wait_send()
         attn_onward(d).wait_send()
-    for w in range(4):
+    for w in range(6):
         for k in range(4):
             w_mate(w, k).wait_send()
-    for w in range(4):
+    for w in range(6):
         for half in range(2):
             w_copy(w, 0, half).wait_send()
             w_copy(w, 1, half).wait_send()
@@ -531,7 +561,7 @@
             pltpu.VMEM((UNITS, 4, *tile), BF16),
             pltpu.VMEM((UNITS, 2, *tile), BF16),
             pltpu.VMEM((4, ROWS, 256), F32),
-            dma((4,)), dma((4, 3, 2)), dma((4, 3, 2)), dma((4, 4)), dma((4, 4)),
+            dma((6,)), dma((6, 3, 2)), dma((6, 3, 2)), dma((6, 4)), dma((6, 4)),
             dma((7,)), dma((7,)), pltpu.SemaphoreType.REGULAR,
             dma((2, 3)), dma((2, 3)), dma((4,)), dma((4,)),
             dma((4,)), dma((4,)), dma((8,)), dma((8,)), dma((3,)), dma((3,)),

time: 124 us -> 120 us (0.968)
  Pallas kernels: 122 us -> 118 us
    pallas_call x1, Pallas kernels: 122 us -> 118 us  [on_device(): pl.pallas_call(kernel, out_shape=jax.ShapeDtypeStruct(tile, BF16), in_spe...]
where the time goes in v4:
time: 120 us
  Pallas kernels  118 us (98%)
  local copies, waits for them, and re-layouts  1.41 us (1%)
    pallas_call x1, Pallas kernels, on_device(): pl.pallas_call(kernel, out_shape=jax.ShapeDtypeStruct(tile, BF16), in_spe...  118 us

profile of v4, /device:TPU:6, one launch (start us, length us, event | category | flops | bytes accessed | tf_op | source)
XLA Modules:
  0.0 119.9 jit_solution(3320807740007295992)
XLA Ops:
  0.0 118.5 %shard_map.73 = bf16[176,128]{1,0:T(8,128)(2,1)} custom-call(bf16[176,128]{1,0:T(8,128)(2,1)} %attn_ref.1, bf16[176,128]{1,0:T(8,128)(2,1)} %res_ref.1, f32[1,128]{1,0:T(1,128)} %bitcast.1, bf16[128,1024]{1,0:T(8,128)(2,1)} %wp_hbm.1, bf16[128,1792]{1,0:T(8,128)(2,1)} %wg_hbm.1, bf16[128,1792]{1,0:T(8,128)(2,1)} %wu_hbm.1, bf16[224,1024]{1,0:T(8,128)(2,1)} %wd_hbm.1), custom_call_target="tpu_custom_call" | custom-call | tf_op jit(solution)/shard_map/pallas_call | solution.py:537
  118.5 1.4 %copy.9 = bf16[176,128]{1,0:T(8,128)(2,1)} copy(bf16[176,128]{1,0:T(8,128)(2,1)} %shard_map.73) | data formatting | bytes 90112

commit v5 on v4

--- a/solution.py
+++ b/solution.py
@@ -12,6 +12,7 @@
 F32, BF16 = jnp.float32, jnp.bfloat16
 X_STEPS = (2, 6, 4)
 PIECES = ((0, 96), (96, 80))
+PARTS = ((0, 64), (64, 64), (128, 48))
 
 
 def rcopy(src, dst, send, recv, **where):
@@ -31,7 +32,7 @@
 def kernel(
     attn_ref, res_ref, gain_ref, wp_hbm, wg_hbm, wu_hbm, wd_hbm, out_ref,
     attn_all, wp, wg, wu, wd, part8, y_send, y_recv, zh_send, zh_recv,
-    gain_recv, stream, scaled, ssq_y, ssq_gy, inv, gu, acc_r, acc_l, hid, down,
+    gain_recv, stream, other, scaled, ssq_y, ssq_gy, inv, gu, acc_r, acc_l, hid, down,
     w_local, w_send, w_recv, w_fsend, w_frecv, a_send, a_recv, hello, ys_send, ys_recv, ya_send, ya_recv,
     sy_send, sy_recv, sg_send, sg_recv, z_send, z_recv, r_send, r_recv, l_send, l_recv,
     h_send, h_recv,
@@ -78,6 +79,8 @@
     signal(barrier, gy=far_gy, gz=across)
     pl.semaphore_wait(barrier, 12)
     signal(hello, gy=far_gy, gz=across)
+    for w in range(6):
+        own_copy(w).wait()
 
     def attn_far():
         return rcopy(attn_ref, attn_all.at[gy], a_send.at[0], a_recv.at[0], gy=far_gy)
@@ -107,15 +110,10 @@
         depth = src.shape[0] // 2
         return dst.at[pl.ds(pl.multiple_of((2 * who + half) * depth, 16), depth), pl.ds(first, width)]
 
-    def own_half(w, half):
-        src, _, first, width = pieces[w]
-        depth = src.shape[0] // 2
-        return src.at[pl.ds(half * depth, depth), pl.ds(first, width)]
-
     def w_copy(w, k, half):
         who = lax.rem(gx + X_STEPS[k], 8)
         return rcopy(
-            own_half(w, half), half_of(w, gx, half), w_send.at[w, k, half], w_recv.at[w, k, half], gx=who
+            half_of(w, gx, half), half_of(w, gx, half), w_send.at[w, k, half], w_recv.at[w, k, half], gx=who
         )
 
     def w_arrival(w, k, half):
@@ -135,8 +133,7 @@
 
     def w_mate(w, k):
         who = gx if k == 3 else lax.rem(gx + 8 - X_STEPS[k], 8)
-        src = own_rows(w) if k == 3 else rows_of(w, who)
-        return rcopy(src, rows_of(w, who), w_fsend.at[w, k], w_frecv.at[w, k], gx=mate)
+        return rcopy(rows_of(w, who), rows_of(w, who), w_fsend.at[w, k], w_frecv.at[w, k], gx=mate)
 
     def w_mate_arrival(w, k):
         who = mate if k == 3 else lax.rem(mate + 8 - X_STEPS[k], 8)
@@ -153,13 +150,19 @@
     for w in range(6):
         w_mate(w, 3).start()
 
-    def pass_weights(w):
+    def pass_onward(w):
         for half in range(2):
             w_arrival(w, half, half).wait_recv()
             w_onward(w, half).start()
+
+    def pass_to_mate(w):
         for k in range(2):
             w_arrival(w, k, 1 - k).wait_recv()
             w_mate(w, k).start()
+
+    def pass_weights(w):
+        pass_onward(w)
+        pass_to_mate(w)
 
     def last_weights(w):
         for half in range(2):
@@ -169,19 +172,19 @@
     def weights_here(w):
         for k in range(4):
             w_mate_arrival(w, k).wait_recv()
-        own_copy(w).wait()
 
     attn_all[gy] = attn_ref[...]
-    attn_far_arrival().wait_recv()
-    for d in range(1, 4):
-        attn_onward(d).start()
-    pass_weights(0)
+    pass_onward(0)
     send_own(1)
     send_own(2)
+    attn_far_arrival().wait_recv()
+    for d in range(1, 4):
+        attn_onward(d).start()
+    pass_to_mate(0)
     pl.semaphore_wait(hello, 1)
 
     def gain_copy():
-        return rcopy(gain_ref, gain_recv, z_send.at[0], z_recv.at[0], gz=across)
+        return rcopy(gain_ref, gain_recv, z_send.at[0, 0], z_recv.at[0, 0], gz=across)
 
     gain_copy().start()
     for d in range(1, 4):
@@ -189,68 +192,69 @@
         attn_arrival(d, True).wait_recv()
     last_weights(0)
 
-    def y_copy(n, d):
-        who = lax.rem(y + d, 4)
+    def y_copy(n, d, p):
+        who, rows = lax.rem(y + d, 4), pl.ds(*PARTS[p])
         return rcopy(
-            y_send.at[n, who], y_recv.at[n, d - 1], ys_send.at[n, d - 1], ys_recv.at[n, d - 1],
-            gz=zh * 4 + who,
+            y_send.at[n, who, :, rows], y_recv.at[n, d - 1, :, rows],
+            ys_send.at[n, d - 1, p], ys_recv.at[n, d - 1, p], gz=zh * 4 + who,
         )
 
-    def keep_tiles(n, m, total):
+    def keep_tiles(n, m, rows, total):
         for half in range(2):
             block = 2 * m + half
             tile = total[:, half * TILE : (half + 1) * TILE]
-            part8[block] = tile
-            y_send[n, block % 4, block // 4] = tile.astype(BF16)
-
-    def y_sum(n, side):
-        total = part8[side * 4 + y]
+            part8[block, rows] = tile
+            y_send[n, block % 4, block // 4, rows] = tile.astype(BF16)
+
+    def y_sum(n, side, rows):
+        total = part8[side * 4 + y, rows]
         for d in range(3):
-            total += y_recv[n, d, side].astype(F32)
+            total += y_recv[n, d, side, rows].astype(F32)
         return total
 
     weights_here(0)
-    for m in range(4):
-        total = None
-        for k in range(4):
-            left = jnp.concatenate([attn_all[2 * k], attn_all[2 * k + 1]], axis=1)
-            term = dot(left, wp[k * 256 : (k + 1) * 256, m * 256 : (m + 1) * 256])
-            total = term if total is None else total + term
-        keep_tiles(0, m, total)
-    for d in range(1, 4):
-        y_copy(0, d).start()
+    for p, part in enumerate(PARTS):
+        rows = pl.ds(*part)
+        for m in range(4):
+            total = None
+            for k in range(4):
+                left = jnp.concatenate([attn_all[2 * k, rows], attn_all[2 * k + 1, rows]], axis=1)
+                term = dot(left, wp[k * 256 : (k + 1) * 256, m * 256 : (m + 1) * 256])
+                total = term if total is None else total + term
+            keep_tiles(0, m, rows, total)
+        for d in range(1, 4):
+            y_copy(0, d, p).start()
     pass_weights(1)
     send_own(3)
-    for d in range(1, 4):
-        y_copy(0, d).wait_recv()
-
-    def zh_copy():
-        return rcopy(zh_send.at[pl.ds(0, 2)], zh_recv.at[pl.ds(0, 2)], z_send.at[1], z_recv.at[1], gz=across)
-
-    mine = res_ref[...].astype(F32) + y_sum(0, zh)
-    theirs = y_sum(0, 1 - zh)
-    zh_send[0] = mine.astype(BF16)
-    zh_send[1] = theirs.astype(BF16)
-    zh_copy().start()
+
+    def zh_copy(p):
+        rows = (pl.ds(0, 2), pl.ds(*PARTS[p]))
+        return rcopy(zh_send.at[rows], zh_recv.at[rows], z_send.at[1, p], z_recv.at[1, p], gz=across)
+
+    for p, part in enumerate(PARTS):
+        rows = pl.ds(*part)
+        for d in range(1, 4):
+            y_copy(0, d, p).wait_recv()
+        mine = res_ref[rows].astype(F32) + y_sum(0, zh, rows)
+        theirs = y_sum(0, 1 - zh, rows)
+        stream[rows], other[rows] = mine, theirs
+        zh_send[0, rows] = mine.astype(BF16)
+        zh_send[1, rows] = theirs.astype(BF16)
+        zh_copy(p).start()
     pass_weights(2)
     send_own(4)
     last_weights(1)
     pass_weights(3)
     gain_copy().wait_recv()
-    zh_copy().wait_recv()
-    mine += zh_recv[1].astype(F32)
-    theirs += zh_recv[0].astype(F32)
-    stream[...] = mine
-    scaled[y, zh] = (mine * gain_ref[...]).astype(BF16)
-    scaled[y, 1 - zh] = (theirs * gain_recv[...]).astype(BF16)
-
-    def scaled_copy(d):
-        who = zh * 4 + lax.rem(y + d, 4)
-        return rcopy(scaled.at[y], scaled.at[y], ya_send.at[d], ya_recv.at[d], gz=who)
-
-    def scaled_arrival(d):
+
+    def scaled_copy(d, p):
+        who, block = zh * 4 + lax.rem(y + d, 4), scaled.at[y, :, pl.ds(*PARTS[p])]
+        return rcopy(block, block, ya_send.at[d, p], ya_recv.at[d, p], gz=who)
+
+    def scaled_arrival(d, p):
         who = lax.rem(y + 4 - d, 4)
-        return rcopy(scaled.at[who], scaled.at[who], ya_send.at[d], ya_recv.at[d], gz=zh * 4 + who)
+        block = scaled.at[who, :, pl.ds(*PARTS[p])]
+        return rcopy(block, block, ya_send.at[d, p], ya_recv.at[d, p], gz=zh * 4 + who)
 
     def ssq_copy(d):
         who = zh * 4 + lax.rem(y + d, 4)
@@ -260,8 +264,17 @@
         who = lax.rem(gy + d, 8)
         return rcopy(ssq_gy.at[0], ssq_gy.at[d], sg_send.at[d], sg_recv.at[d], gy=who)
 
-    for d in range(1, 4):
-        scaled_copy(d).start()
+    for p, part in enumerate(PARTS):
+        rows = pl.ds(*part)
+        zh_copy(p).wait_recv()
+        mine = stream[rows] + zh_recv[1, rows].astype(F32)
+        theirs = other[rows] + zh_recv[0, rows].astype(F32)
+        stream[rows], other[rows] = mine, theirs
+        scaled[y, zh, rows] = (mine * gain_ref[...]).astype(BF16)
+        scaled[y, 1 - zh, rows] = (theirs * gain_recv[...]).astype(BF16)
+        for d in range(1, 4):
+            scaled_copy(d, p).start()
+    mine, theirs = stream[...], other[...]
     squares = jnp.sum(mine * mine + theirs * theirs, axis=1, keepdims=True)
     squares = jnp.concatenate(
         [jnp.broadcast_to(squares, (ROWS, TILE)), jnp.zeros((256 - ROWS, TILE), F32)], axis=0
@@ -273,7 +286,8 @@
     pass_weights(4)
     send_own(5)
     for d in range(1, 4):
-        scaled_arrival(d).wait_recv()
+        for p in range(len(PARTS)):
+            scaled_arrival(d, p).wait_recv()
         ssq_copy(d).wait_recv()
     ssq_gy[0] = (ssq_y[0] + ssq_y[1] + ssq_y[2] + ssq_y[3])[:1]
     for d in range(1, 8):
@@ -296,7 +310,7 @@
                 term = dot(left, w[k * 256 : (k + 1) * 256, columns])
                 total = term if total is None else total + term
             for half in range(2):
-                gu[unit, 2 * part + half] = total[:, half * TILE : (half + 1) * TILE]
+                gu[unit, 2 * half + part] = total[:, half * TILE : (half + 1) * TILE]
 
     def r_copy(unit, part):
         return rcopy(
@@ -334,11 +348,11 @@
             weights_here(4)
 
         for tile in range(4):
-            if tile % 2 == 0:
+            if tile == 0:
 
                 @pl.when(t < 4)
                 def _():
-                    products(lax.select(gy < 4, 6 - t, t), (tile // 2,))
+                    products(lax.select(gy < 4, 6 - t, t))
 
             @pl.when(jnp.logical_and(t >= gy, owner_of(right) > gy))
             def _():
@@ -383,25 +397,6 @@
     owns = gy != 4
     own_unit = gy - lax.min(lax.max(gy - 4, 0), 1)
 
-    @pl.when(owns)
-    def _():
-        for tile in range(4):
-
-            @pl.when(gy > 0)
-            def _():
-                r_copy(own_unit, tile).wait_recv()
-                gu[own_unit, tile] += acc_r[own_unit, tile].astype(F32)
-
-            @pl.when(gy < 7)
-            def _():
-                l_copy(own_unit, tile).wait_recv()
-                gu[own_unit, tile] += acc_l[own_unit, tile].astype(F32)
-
-        for half in range(2):
-            gate = inv[:ROWS] * gu[own_unit, half]
-            up = inv[:ROWS] * gu[own_unit, 2 + half]
-            hid[own_unit, half] = (gate / (1.0 + jnp.exp(-gate)) * up).astype(BF16)
-
     weights_here(5)
 
     def hidden_copy(unit, k, side, hop):
@@ -428,9 +423,25 @@
 
     @pl.when(owns)
     def _():
-        for k in range(4):
-            for side in range(2):
-                hidden_sends(own_unit, k, side, lambda copy: copy.start())
+        for half in range(2):
+            for tile in (2 * half, 2 * half + 1):
+
+                @pl.when(gy > 0)
+                def _():
+                    r_copy(own_unit, tile).wait_recv()
+                    gu[own_unit, tile] += acc_r[own_unit, tile].astype(F32)
+
+                @pl.when(gy < 7)
+                def _():
+                    l_copy(own_unit, tile).wait_recv()
+                    gu[own_unit, tile] += acc_l[own_unit, tile].astype(F32)
+
+            gate = inv[:ROWS] * gu[own_unit, 2 * half]
+            up = inv[:ROWS] * gu[own_unit, 2 * half + 1]
+            hid[own_unit, half] = (gate / (1.0 + jnp.exp(-gate)) * up).astype(BF16)
+            for k in (2 * half, 2 * half + 1):
+                for side in range(2):
+                    hidden_sends(own_unit, k, side, lambda copy: copy.start())
 
         add_down(own_unit)
 
@@ -468,22 +479,23 @@
 
     lax.fori_loop(1, 5, hidden_step, 0)
 
-    for m in range(4):
-        keep_tiles(1, m, down[m])
-    for d in range(1, 4):
-        y_copy(1, d).start()
-    for d in range(1, 4):
-        y_copy(1, d).wait_recv()
-
-    def last_copy():
-        return rcopy(zh_send.at[2], zh_recv.at[2], z_send.at[2], z_recv.at[2], gz=across)
-
-    zh_send[2] = y_sum(1, 1 - zh).astype(BF16)
-    last_copy().start()
-    stream[...] += y_sum(1, zh)
-    last_copy().wait_recv()
-    out_ref[...] = (stream[...] + zh_recv[2].astype(F32)).astype(BF16)
-
+    def last_copy(p):
+        rows = pl.ds(*PARTS[p])
+        return rcopy(zh_send.at[2, rows], zh_recv.at[2, rows], z_send.at[2, p], z_recv.at[2, p], gz=across)
+
+    for p, part in enumerate(PARTS):
+        rows = pl.ds(*part)
+        for m in range(4):
+            keep_tiles(1, m, rows, down[m, rows])
+        for d in range(1, 4):
+            y_copy(1, d, p).start()
+    for p, part in enumerate(PARTS):
+        rows = pl.ds(*part)
+        for d in range(1, 4):
+            y_copy(1, d, p).wait_recv()
+        zh_send[2, rows] = y_sum(1, 1 - zh, rows).astype(BF16)
+        last_copy(p).start()
+        stream[rows] += y_sum(1, zh, rows)
     for d in range(1, 8):
         ssq_gy_copy(d).wait_send()
     attn_far().wait_send()
@@ -499,13 +511,13 @@
             w_copy(w, 1, half).wait_send()
             w_onward(w, half).wait_send()
     for d in range(1, 4):
-        y_copy(0, d).wait_send()
-        y_copy(1, d).wait_send()
-        scaled_copy(d).wait_send()
+        for p in range(len(PARTS)):
+            y_copy(0, d, p).wait_send()
+            scaled_copy(d, p).wait_send()
         ssq_copy(d).wait_send()
     gain_copy().wait_send()
-    zh_copy().wait_send()
-    last_copy().wait_send()
+    for p in range(len(PARTS)):
+        zh_copy(p).wait_send()
 
     def drain(unit, carry):
         owner = owner_of(unit)
@@ -528,6 +540,15 @@
         return carry
 
     lax.fori_loop(0, UNITS, drain, 0)
+
+    for p, part in enumerate(PARTS):
+        rows = pl.ds(*part)
+        last_copy(p).wait_recv()
+        out_ref[rows] = (stream[rows] + zh_recv[2, rows].astype(F32)).astype(BF16)
+    for p in range(len(PARTS)):
+        last_copy(p).wait_send()
+        for d in range(1, 4):
+            y_copy(1, d, p).wait_send()
 
 
 def on_device(attn_out, residual, proj_weight, norm_gain, gate_proj, up_proj, down_proj):
@@ -552,6 +573,7 @@
             pltpu.VMEM((3, *tile), BF16),
             pltpu.VMEM((1, TILE), F32),
             pltpu.VMEM(tile, F32),
+            pltpu.VMEM(tile, F32),
             pltpu.VMEM((4, 2, *tile), BF16),
             pltpu.VMEM((4, 8, 256), F32),
             pltpu.VMEM((8, 1, 256), F32),
@@ -563,8 +585,8 @@
             pltpu.VMEM((4, ROWS, 256), F32),
             dma((6,)), dma((6, 3, 2)), dma((6, 3, 2)), dma((6, 4)), dma((6, 4)),
             dma((7,)), dma((7,)), pltpu.SemaphoreType.REGULAR,
-            dma((2, 3)), dma((2, 3)), dma((4,)), dma((4,)),
-            dma((4,)), dma((4,)), dma((8,)), dma((8,)), dma((3,)), dma((3,)),
+            dma((2, 3, len(PARTS))), dma((2, 3, len(PARTS))), dma((4, len(PARTS))), dma((4, len(PARTS))),
+            dma((4,)), dma((4,)), dma((8,)), dma((8,)), dma((3, len(PARTS))), dma((3, len(PARTS))),
             dma((UNITS, 4)), dma((UNITS, 4)), dma((UNITS, 4)), dma((UNITS, 4)),
             dma((UNITS, 2, 2, 4)), dma((UNITS, 4)),
         ],

time: 120 us -> 116 us (0.967)
  Pallas kernels: 118 us -> 115 us
    pallas_call x1, Pallas kernels: 118 us -> 115 us  [on_device(): pl.pallas_call(kernel, out_shape=jax.ShapeDtypeStruct(tile, BF16), in_spe...]
where the time goes in v5:
time: 116 us
  Pallas kernels  115 us (99%)
  local copies, waits for them, and re-layouts  1.41 us (1%)
    pallas_call x1, Pallas kernels, on_device(): pl.pallas_call(kernel, out_shape=jax.ShapeDtypeStruct(tile, BF16), in_spe...  115 us

profile of v5, /device:TPU:6, one launch (start us, length us, event | category | flops | bytes accessed | tf_op | source)
XLA Modules:
  0.0 116.0 jit_solution(17301949733228741650)
XLA Ops:
  0.0 114.5 %shard_map.73 = bf16[176,128]{1,0:T(8,128)(2,1)} custom-call(bf16[176,128]{1,0:T(8,128)(2,1)} %attn_ref.1, bf16[176,128]{1,0:T(8,128)(2,1)} %res_ref.1, f32[1,128]{1,0:T(1,128)} %bitcast.1, bf16[128,1024]{1,0:T(8,128)(2,1)} %wp_hbm.1, bf16[128,1792]{1,0:T(8,128)(2,1)} %wg_hbm.1, bf16[128,1792]{1,0:T(8,128)(2,1)} %wu_hbm.1, bf16[224,1024]{1,0:T(8,128)(2,1)} %wd_hbm.1), custom_call_target="tpu_custom_call" | custom-call | tf_op jit(solution)/shard_map/pallas_call | solution.py:558
  114.5 1.4 %copy.9 = bf16[176,128]{1,0:T(8,128)(2,1)} copy(bf16[176,128]{1,0:T(8,128)(2,1)} %shard_map.73) | data formatting | bytes 90112

commit v6 on v5

--- a/solution.py
+++ b/solution.py
@@ -30,10 +30,10 @@
 
 
 def kernel(
-    attn_ref, res_ref, gain_ref, wp_hbm, wg_hbm, wu_hbm, wd_hbm, out_ref,
-    attn_all, wp, wg, wu, wd, part8, y_send, y_recv, zh_send, zh_recv,
+    attn_hbm, res_hbm, gain_hbm, wp_hbm, wg_hbm, wu_hbm, wd_hbm, out_ref,
+    attn_all, res_ref, gain_ref, wp, wg, wu, wd, part8, y_send, y_recv, zh_send, zh_recv,
     gain_recv, stream, other, scaled, ssq_y, ssq_gy, inv, gu, acc_r, acc_l, hid, down,
-    w_local, w_send, w_recv, w_fsend, w_frecv, a_send, a_recv, hello, ys_send, ys_recv, ya_send, ya_recv,
+    w_local, w_send, w_recv, w_fsend, w_frecv, a_send, a_recv, f_send, f_recv, hello, ys_send, ys_recv, ya_send, ya_recv,
     sy_send, sy_recv, sg_send, sg_recv, z_send, z_recv, r_send, r_recv, l_send, l_recv,
     h_send, h_recv,
 ):
@@ -60,8 +60,9 @@
     def own_copy(w):
         return pltpu.make_async_copy(own_rows(w), rows_of(w, gx), w_local.at[w])
 
-    for w in range(6):
-        own_copy(w).start()
+    def local(k):
+        src, dst = ((attn_hbm, attn_all.at[gy]), (res_hbm, res_ref), (gain_hbm, gain_ref))[k]
+        return pltpu.make_async_copy(src, dst, w_local.at[6 + k])
 
     far_gy, quad, place = lax.rem(gy + 4, 8), gy // 4 * 4, lax.rem(gy, 4)
 
@@ -77,31 +78,44 @@
         signal(barrier, gy=in_quad(d))
     signal(barrier, gy=far_gy)
     signal(barrier, gy=far_gy, gz=across)
+    for k in range(3):
+        local(k).start()
+    for w in range(6):
+        own_copy(w).start()
+    for k in range(3):
+        local(k).wait()
     pl.semaphore_wait(barrier, 12)
     signal(hello, gy=far_gy, gz=across)
     for w in range(6):
         own_copy(w).wait()
 
-    def attn_far():
-        return rcopy(attn_ref, attn_all.at[gy], a_send.at[0], a_recv.at[0], gy=far_gy)
-
-    def attn_far_arrival():
-        return rcopy(attn_ref, attn_all.at[far_gy], a_send.at[0], a_recv.at[0], gy=far_gy)
+    def attn_far(p):
+        rows = pl.ds(*PIECES[p])
+        return rcopy(attn_all.at[gy, rows], attn_all.at[gy, rows], f_send.at[0, p], f_recv.at[0, p], gy=far_gy)
+
+    def attn_far_arrival(p):
+        rows = pl.ds(*PIECES[p])
+        return rcopy(attn_all.at[far_gy, rows], attn_all.at[far_gy, rows], f_send.at[0, p], f_recv.at[0, p], gy=far_gy)
 
     def attn_near(d):
-        return rcopy(attn_ref, attn_all.at[gy], a_send.at[d], a_recv.at[d], gy=in_quad(d))
-
-    def attn_onward(d):
-        block = attn_all.at[far_gy]
-        return rcopy(block, block, a_send.at[3 + d], a_recv.at[3 + d], gy=in_quad(d))
-
-    def attn_arrival(d, onward):
+        return rcopy(attn_all.at[gy], attn_all.at[gy], a_send.at[d], a_recv.at[d], gy=in_quad(d))
+
+    def attn_onward(d, p):
+        block = attn_all.at[far_gy, pl.ds(*PIECES[p])]
+        return rcopy(block, block, f_send.at[d, p], f_recv.at[d, p], gy=in_quad(d))
+
+    def attn_arrival(d):
         who = in_quad(4 - d)
-        block = attn_all.at[lax.rem(who + 4, 8) if onward else who]
-        k = d + 3 if onward else d
-        return rcopy(block, block, a_send.at[k], a_recv.at[k], gy=who)
-
-    attn_far().start()
+        block = attn_all.at[who]
+        return rcopy(block, block, a_send.at[d], a_recv.at[d], gy=who)
+
+    def attn_onward_arrival(d, p):
+        who = in_quad(4 - d)
+        block = attn_all.at[lax.rem(who + 4, 8), pl.ds(*PIECES[p])]
+        return rcopy(block, block, f_send.at[d, p], f_recv.at[d, p], gy=who)
+
+    for p in range(2):
+        attn_far(p).start()
     for d in range(1, 4):
         attn_near(d).start()
 
@@ -173,13 +187,13 @@
         for k in range(4):
             w_mate_arrival(w, k).wait_recv()
 
-    attn_all[gy] = attn_ref[...]
     pass_onward(0)
     send_own(1)
     send_own(2)
-    attn_far_arrival().wait_recv()
-    for d in range(1, 4):
-        attn_onward(d).start()
+    for p in range(2):
+        attn_far_arrival(p).wait_recv()
+        for d in range(1, 4):
+            attn_onward(d, p).start()
     pass_to_mate(0)
     pl.semaphore_wait(hello, 1)
 
@@ -188,8 +202,9 @@
 
     gain_copy().start()
     for d in range(1, 4):
-        attn_arrival(d, False).wait_recv()
-        attn_arrival(d, True).wait_recv()
+        attn_arrival(d).wait_recv()
+        for p in range(2):
+            attn_onward_arrival(d, p).wait_recv()
     last_weights(0)
 
     def y_copy(n, d, p):
@@ -366,12 +381,9 @@
         def _():
             products(lax.select(gy < 4, t, 6 - t))
 
-        @pl.when(t == 0)
+        @pl.when(t == 1)
         def _():
             last_weights(3)
-
-        @pl.when(t == 1)
-        def _():
             last_weights(4)
 
         @pl.when(t == 3)
@@ -498,10 +510,12 @@
         stream[rows] += y_sum(1, zh, rows)
     for d in range(1, 8):
         ssq_gy_copy(d).wait_send()
-    attn_far().wait_send()
+    for p in range(2):
+        attn_far(p).wait_send()
     for d in range(1, 4):
         attn_near(d).wait_send()
-        attn_onward(d).wait_send()
+        for p in range(2):
+            attn_onward(d, p).wait_send()
     for w in range(6):
         for k in range(4):
             w_mate(w, k).wait_send()
@@ -558,10 +572,12 @@
     return pl.pallas_call(
         kernel,
         out_shape=jax.ShapeDtypeStruct(tile, BF16),
-        in_specs=[in_vmem] * 3 + [in_hbm] * 4,
+        in_specs=[in_hbm] * 7,
         out_specs=in_vmem,
         scratch_shapes=[
             pltpu.VMEM((8, *tile), BF16),
+            pltpu.VMEM(tile, BF16),
+            pltpu.VMEM((1, TILE), F32),
             pltpu.VMEM((1024, 1024), BF16),
             pltpu.VMEM((1024, 1792), BF16),
             pltpu.VMEM((1024, 1792), BF16),
@@ -583,8 +599,8 @@
             pltpu.VMEM((UNITS, 4, *tile), BF16),
             pltpu.VMEM((UNITS, 2, *tile), BF16),
             pltpu.VMEM((4, ROWS, 256), F32),
-            dma((6,)), dma((6, 3, 2)), dma((6, 3, 2)), dma((6, 4)), dma((6, 4)),
-            dma((7,)), dma((7,)), pltpu.SemaphoreType.REGULAR,
+            dma((9,)), dma((6, 3, 2)), dma((6, 3, 2)), dma((6, 4)), dma((6, 4)),
+            dma((4,)), dma((4,)), dma((4, 2)), dma((4, 2)), pltpu.SemaphoreType.REGULAR,
             dma((2, 3, len(PARTS))), dma((2, 3, len(PARTS))), dma((4, len(PARTS))), dma((4, len(PARTS))),
             dma((4,)), dma((4,)), dma((8,)), dma((8,)), dma((3, len(PARTS))), dma((3, len(PARTS))),
             dma((UNITS, 4)), dma((UNITS, 4)), dma((UNITS, 4)), dma((UNITS, 4)),

time: 116 us -> 116 us (level)
  no operation moved by 1% of the time
where the time goes in v6:
time: 116 us; the launch traced here: 115 us
  Pallas kernels  114 us (98%)
  local copies, waits for them, and re-layouts  1.41 us (1%)
    pallas_call x1, Pallas kernels, on_device(): pl.pallas_call(kernel, out_shape=jax.ShapeDtypeStruct(tile, BF16), in_spe...  114 us

profile of v6, /device:TPU:6, one launch (start us, length us, event | category | flops | bytes accessed | tf_op | source)
XLA Modules:
  0.0 115.1 jit_solution(6327550681364429054)
XLA Ops:
  0.0 113.7 %shard_map.73 = bf16[176,128]{1,0:T(8,128)(2,1)} custom-call(bf16[176,128]{1,0:T(8,128)(2,1)} %attn_hbm.1, bf16[176,128]{1,0:T(8,128)(2,1)} %res_hbm.1, f32[1,128]{1,0:T(1,128)} %bitcast.1, bf16[128,1024]{1,0:T(8,128)(2,1)} %wp_hbm.1, bf16[128,1792]{1,0:T(8,128)(2,1)} %wg_hbm.1, bf16[128,1792]{1,0:T(8,128)(2,1)} %wu_hbm.1, bf16[224,1024]{1,0:T(8,128)(2,1)} %wd_hbm.1), custom_call_target="tpu_custom_call" | custom-call | tf_op jit(solution)/shard_map/pallas_call | solution.py:572
  113.7 1.4 %copy.9 = bf16[176,128]{1,0:T(8,128)(2,1)} copy(bf16[176,128]{1,0:T(8,128)(2,1)} %shard_map.73) | data formatting | bytes 90112
